TPU v7x, 128 devices: a whole 4x4x4 slice. The times are simulated.
128 devices in a mesh: seg: 64 (over y, z_hi, x, core), freq: 2 (over z_lo).
Axes of the slice: x: 4, y: 4, z: 4 (z_hi: 2, z_lo: 2; z = z_hi * 2 + z_lo), core: 2. Of those that a mesh axis runs over, the one named last changes fastest.
Arguments:
- coarse: float32 [256, 512, 2048], P('seg', None, 'freq'), may hold values from 0.5 to 8
- offsets: int32 [256, 32], replicated, may hold values from -8 to 8, as said below
Outputs:
- fine: float32 [32, 512, 2048], P(None, 'seg', 'freq')
- peaks: float32 [512], P('seg')
Inputs may be any that keep to these rules, and one draw needn't show every extreme that they name: `offsets`: every entry lies in -8 to 8, and both ends occur in every draw.
All inputs are finite; a program needn't handle non-finite values.
Results may differ from a plain program's by a relative error of at most 0.0003.
Values sent between devices are 32-bit elements; how exact they have to be, the bound alone decides.
No kernel may reach another device: no remote copies, remote signals or barrier semaphores. Data moves between devices by JAX's collectives and lax.ppermute only.
A program may use at most 128 MiB of HBM per device.

v0:
```python
import jax
import jax.numpy as jnp
from jax import lax
from jax.sharding import PartitionSpec as P

HALO = 8


def extended(block, sides, width):
    for axis, dim in sides:
        count = lax.axis_size(axis)
        forward = [(i, i + 1) for i in range(count - 1)]
        backward = [(target, source) for source, target in forward]
        low = lax.ppermute(
            lax.slice_in_dim(block, block.shape[dim] - width, None, axis=dim), axis, forward
        )
        high = lax.ppermute(lax.slice_in_dim(block, 0, width, axis=dim), axis, backward)
        block = jnp.concatenate([low, block, high], axis=dim)
    return block


def shift_sum(padded, offsets):
    seg_count, point_count, wide_bins = padded.shape
    bin_count = wide_bins - 2 * HALO
    spin_count = offsets.shape[1]
    columns = offsets.T
    total = jnp.zeros((spin_count, point_count, bin_count), jnp.float32)
    for shift in range(-HALO, HALO + 1):
        weights = (columns == shift).astype(jnp.float32) / seg_count
        product = jnp.einsum(
            "ks,spw->kpw",
            weights,
            padded,
            precision=lax.Precision.HIGHEST,
            preferred_element_type=jnp.float32,
        )
        total = total + product[:, :, HALO + shift : HALO + shift + bin_count]
    return total


def on_device(coarse, offsets):
    nseg = lax.axis_size("seg")
    local_segs, points, bins_local = coarse.shape
    blocks = coarse.reshape(local_segs, nseg, points // nseg, bins_local)
    maps = lax.all_to_all(blocks, "seg", split_axis=1, concat_axis=0, tiled=True)[:, 0]
    padded = extended(maps, (("freq", 2),), HALO)
    fine_part = shift_sum(padded, offsets)
    top = jnp.max(fine_part, axis=(0, 2))
    top_rows = top[None, :]
    peaks = lax.pmax(top_rows[0], "freq")
    return (fine_part, peaks)


def solution(mesh):
    return jax.shard_map(
        on_device,
        mesh=mesh,
        in_specs=(P("seg", None, "freq"), P()),
        out_specs=(P(None, "seg", "freq"), P("seg")),
        check_vma=False,
    )
```

profile of v0, /device:TPU:0, one launch (start us, length us, event | category | flops | bytes accessed | tf_op | source)
XLA Modules:
  0.0 281.8 jit_solution(17570341755489511245)
XLA Ops:
  0.6 4.2 %copy.15 = f32[4,64,8,1024]{3,2,0,1:T(8,128)S(1)} copy(f32[4,64,8,1024]{3,2,1,0:T(8,128)} %bitcast.60) | data formatting | bytes 16777216 | tf_op jit(solution)/shard_map/reshape | solution.py:44
  4.9 109.2 %all_to_all.15 = f32[4,64,8,1024]{3,2,0,1:T(8,128)} all-to-all(f32[4,64,8,1024]{3,2,0,1:T(8,128)S(1)} %copy.15), channel_id=1, replica_groups=mesh['seg'=64,'freq'=2] {'seg'}, dimensions={1} | all-to-all | bytes 16777216 | tf_op jit(solution)/shard_map/all_to_all | solution.py:45
  114.0 9.2 %copy.16 = f32[256,8,1024]{0,2,1:T(8,128)} copy(f32[256,8,1024]{2,1,0:T(8,128)} %bitcast.59) | data formatting | bytes 16777216 | tf_op jit(solution)/shard_map/squeeze | solution.py:45
  123.2 0.9 fusion.235
  124.1 2.9 %collective-permute-start = (f32[256,8,8]{0,2,1:T(8,128)S(1)}, f32[256,8,8]{0,2,1:T(8,128)S(1)}, u32[]{:S(2)}, u32[]{:S(2)}) collective-permute-start(f32[256,8,8]{0,2,1:T(8,128)S(1)} %get-tuple-element.10), channel_id=1, source_target_pairs={{0,1},{2,3},{4,5},{6,7},{8,9},{10,11},{12,13},{14,15},{16,17},{18,... | collective-permute-start | bytes 196616 | tf_op jit(solution)/shard_map/ppermute | solution.py:14
  127.0 0.0 copy-start
  127.0 1.3 collective-permute-start.1
  128.3 0.6 collective-permute-done
  128.9 4.3 %collective-permute-done.1 = f32[256,8,8]{0,2,1:T(8,128)S(1)} collective-permute-done((f32[256,8,8]{0,2,1:T(8,128)S(1)}, f32[256,8,8]{0,2,1:T(8,128)S(1)}, u32[]{:S(2)}, u32[]{:S(2)}) %collective-permute-start.1) | collective-permute-done | bytes 65568 | tf_op jit(solution)/shard_map/ppermute | solution.py:17
  133.2 4.3 %pad_maximum_fusion = f32[256,8,1040]{0,2,1:T(8,128)S(1)} fusion(f32[256,8,8]{0,2,1:T(8,128)S(1)} %collective-permute-done.1, f32[256,8,1024]{0,2,1:T(8,128)} %copy.16, f32[256,8,8]{0,2,1:T(8,128)S(1)} %collective-permute-done), kind=kLoop, calls=%fused_computation | loop fusion | flops 4259840 | bytes 17039360 | tf_op jit(solution)/shard_map/concatenate | solution.py:18
  137.5 0.0 copy-done
  137.5 7.7 %fusion = f32[32,8,1024]{2,0,1:T(8,128)S(1)} fusion(f32[256,8,1040]{0,2,1:T(8,128)S(1)} %pad_maximum_fusion, s32[256,32]{0,1:T(8,128)S(1)} %copy-done), kind=kOutput, calls=%fused_computation.1 | convolution fusion | flops 805322752 | bytes 9469952 | tf_op jit(solution)/shard_map/ks,spw->kpw/dot_general | solution.py:30
  145.2 7.6 %fusion.2 = f32[32,8,1024]{2,0,1:T(8,128)S(1)} fusion(f32[256,8,1040]{0,2,1:T(8,128)S(1)} %pad_maximum_fusion, s32[256,32]{0,1:T(8,128)S(1)} %copy-done), kind=kOutput, calls=%fused_computation.3 | convolution fusion | flops 805322752 | bytes 9469952 | tf_op jit(solution)/shard_map/ks,spw->kpw/dot_general | solution.py:30
  152.8 7.7 %fusion.4 = f32[32,8,1024]{2,0,1:T(8,128)S(1)} fusion(f32[256,8,1040]{0,2,1:T(8,128)S(1)} %pad_maximum_fusion, s32[256,32]{0,1:T(8,128)S(1)} %copy-done), kind=kOutput, calls=%fused_computation.5 | convolution fusion | flops 805322752 | bytes 9469952 | tf_op jit(solution)/shard_map/ks,spw->kpw/dot_general | solution.py:30
  160.5 7.6 %fusion.6 = f32[32,8,1024]{2,0,1:T(8,128)S(1)} fusion(f32[256,8,1040]{0,2,1:T(8,128)S(1)} %pad_maximum_fusion, s32[256,32]{0,1:T(8,128)S(1)} %copy-done), kind=kOutput, calls=%fused_computation.7 | convolution fusion | flops 805322752 | bytes 9469952 | tf_op jit(solution)/shard_map/ks,spw->kpw/dot_general | solution.py:30
  168.1 7.8 %fusion.8 = f32[32,8,1024]{2,0,1:T(8,128)S(1)} fusion(f32[256,8,1040]{0,2,1:T(8,128)S(1)} %pad_maximum_fusion, s32[256,32]{0,1:T(8,128)S(1)} %copy-done), kind=kOutput, calls=%fused_computation.9 | convolution fusion | flops 805322752 | bytes 9469952 | tf_op jit(solution)/shard_map/ks,spw->kpw/dot_general | solution.py:30
  175.9 7.6 %fusion.10 = f32[32,8,1024]{2,0,1:T(8,128)S(1)} fusion(f32[256,8,1040]{0,2,1:T(8,128)S(1)} %pad_maximum_fusion, s32[256,32]{0,1:T(8,128)S(1)} %copy-done), kind=kOutput, calls=%fused_computation.11 | convolution fusion | flops 805322752 | bytes 9469952 | tf_op jit(solution)/shard_map/ks,spw->kpw/dot_general | solution.py:30
  183.5 7.6 %fusion.12 = f32[32,8,1024]{2,0,1:T(8,128)S(1)} fusion(f32[256,8,1040]{0,2,1:T(8,128)S(1)} %pad_maximum_fusion, s32[256,32]{0,1:T(8,128)S(1)} %copy-done), kind=kOutput, calls=%fused_computation.13 | convolution fusion | flops 805322752 | bytes 9469952 | tf_op jit(solution)/shard_map/ks,spw->kpw/dot_general | solution.py:30
  191.0 8.0 %fusion.14 = f32[32,8,1024]{2,0,1:T(8,128)S(1)} fusion(f32[256,8,1040]{0,2,1:T(8,128)S(1)} %pad_maximum_fusion, s32[256,32]{0,1:T(8,128)S(1)} %copy-done), kind=kOutput, calls=%fused_computation.15 | convolution fusion | flops 805322752 | bytes 9469952 | tf_op jit(solution)/shard_map/ks,spw->kpw/dot_general | solution.py:30
  199.0 7.7 %fusion.16 = f32[32,8,1024]{2,0,1:T(8,128)S(1)} fusion(f32[256,8,1040]{0,2,1:T(8,128)S(1)} %pad_maximum_fusion, s32[256,32]{0,1:T(8,128)S(1)} %copy-done), kind=kOutput, calls=%fused_computation.17 | convolution fusion | flops 805322752 | bytes 9469952 | tf_op jit(solution)/shard_map/ks,spw->kpw/dot_general | solution.py:30
  206.8 8.7 %fusion.18 = f32[32,8,1024]{2,0,1:T(8,128)} fusion(f32[256,8,1040]{0,2,1:T(8,128)S(1)} %pad_maximum_fusion, s32[256,32]{0,1:T(8,128)S(1)} %copy-done), kind=kOutput, calls=%fused_computation.19 | convolution fusion | flops 805322752 | bytes 9469952 | tf_op jit(solution)/shard_map/ks,spw->kpw/dot_general | solution.py:30
  215.5 8.6 %fusion.20 = f32[32,8,1024]{2,0,1:T(8,128)} fusion(f32[256,8,1040]{0,2,1:T(8,128)S(1)} %pad_maximum_fusion, s32[256,32]{0,1:T(8,128)S(1)} %copy-done), kind=kOutput, calls=%fused_computation.21 | convolution fusion | flops 805322752 | bytes 9469952 | tf_op jit(solution)/shard_map/ks,spw->kpw/dot_general | solution.py:30
  224.1 8.8 %fusion.22 = f32[32,8,1024]{2,0,1:T(8,128)} fusion(f32[256,8,1040]{0,2,1:T(8,128)S(1)} %pad_maximum_fusion, s32[256,32]{0,1:T(8,128)S(1)} %copy-done), kind=kOutput, calls=%fused_computation.23 | convolution fusion | flops 805322752 | bytes 9469952 | tf_op jit(solution)/shard_map/ks,spw->kpw/dot_general | solution.py:30
  232.9 8.6 %fusion.24 = f32[32,8,1024]{2,0,1:T(8,128)} fusion(f32[256,8,1040]{0,2,1:T(8,128)S(1)} %pad_maximum_fusion, s32[256,32]{0,1:T(8,128)S(1)} %copy-done), kind=kOutput, calls=%fused_computation.25 | convolution fusion | flops 805322752 | bytes 9469952 | tf_op jit(solution)/shard_map/ks,spw->kpw/dot_general | solution.py:30
  241.4 7.6 %fusion.26 = f32[32,8,1024]{2,0,1:T(8,128)S(1)} fusion(f32[256,8,1040]{0,2,1:T(8,128)S(1)} %pad_maximum_fusion, s32[256,32]{0,1:T(8,128)S(1)} %copy-done), kind=kOutput, calls=%fused_computation.27 | convolution fusion | flops 805322752 | bytes 9469952 | tf_op jit(solution)/shard_map/ks,spw->kpw/dot_general | solution.py:30
  249.0 8.0 %fusion.28 = f32[32,8,1024]{2,0,1:T(8,128)S(1)} fusion(f32[256,8,1040]{0,2,1:T(8,128)S(1)} %pad_maximum_fusion, s32[256,32]{0,1:T(8,128)S(1)} %copy-done), kind=kOutput, calls=%fused_computation.29 | convolution fusion | flops 805322752 | bytes 9469952 | tf_op jit(solution)/shard_map/ks,spw->kpw/dot_general | solution.py:30
  257.0 7.6 %fusion.30 = f32[32,8,1024]{2,0,1:T(8,128)S(1)} fusion(f32[256,8,1040]{0,2,1:T(8,128)S(1)} %pad_maximum_fusion, s32[256,32]{0,1:T(8,128)S(1)} %copy-done), kind=kOutput, calls=%fused_computation.31 | convolution fusion | flops 805322752 | bytes 9469952 | tf_op jit(solution)/shard_map/ks,spw->kpw/dot_general | solution.py:30
  264.6 10.0 %fusion.236 = (f32[8]{0:T(128)S(1)}, f32[32,8,1024]{2,0,1:T(8,128)S(1)}) fusion(f32[32,8,1024]{2,0,1:T(8,128)S(1)} %fusion, f32[32,8,1024]{2,0,1:T(8,128)S(1)} %fusion.2, f32[32,8,1024]{2,0,1:T(8,128)S(1)} %fusion.4, f32[32,8,1024]{2,0,1:T(8,128)S(1)} %fusion.6, f32[32,8,1024]{2,0,1:T(8,128)S(1)} %fusion.8, f32[32,8,1024]{2,0,1:T(8,128)S(1)} %fusion.10, ...), kind=kOutput, calls=%fused_computation.205 | convolution fusion | flops 809779200 | bytes 26247200 | tf_op jit(solution)/shard_map/ks,spw->kpw/dot_general | solution.py:30
  274.6 5.4 %pmax.7 = f32[8]{0:T(128)} all-reduce(f32[8]{0:T(128)S(1)} %get-tuple-element.12), channel_id=1, replica_groups=mesh['seg'=64,'freq'=2] {'freq'}, use_global_device_ids=true, to_apply=%region_1.0 | all-reduce | flops 8 | bytes 64 | tf_op jit(solution)/shard_map/pmax | solution.py:50
  280.0 1.6 copy.19
Async XLA Ops:
  124.1 4.8 %collective-permute-start = (f32[256,8,8]{0,2,1:T(8,128)S(1)}, f32[256,8,8]{0,2,1:T(8,128)S(1)}, u32[]{:S(2)}, u32[]{:S(2)}) collective-permute-start(f32[256,8,8]{0,2,1:T(8,128)S(1)} %get-tuple-element.10), channel_id=1, source_target_pairs={{0,1},{2,3},{4,5},{6,7},{8,9},{10,11},{12,13},{14,15},{16,17},{18,... | collective-permute-start | bytes 196616 | tf_op jit(solution)/shard_map/ppermute | solution.py:14
  127.0 10.5 %copy-start = (s32[256,32]{0,1:T(8,128)S(1)}, s32[256,32]{0,1:T(8,128)}, u32[]{:S(2)}) copy-start(s32[256,32]{0,1:T(8,128)} %param.3) | copy-start | bytes 98308
  127.0 6.2 %collective-permute-start.1 = (f32[256,8,8]{0,2,1:T(8,128)S(1)}, f32[256,8,8]{0,2,1:T(8,128)S(1)}, u32[]{:S(2)}, u32[]{:S(2)}) collective-permute-start(f32[256,8,8]{0,2,1:T(8,128)S(1)} %get-tuple-element.11), channel_id=1, source_target_pairs={{1,0},{3,2},{5,4},{7,6},{9,8},{11,10},{13,12},{15,14},{17,16},{19,... | collective-permute-start | bytes 196616 | tf_op jit(solution)/shard_map/ppermute | solution.py:17
where the time goes:
time: 285 us; the launch traced here: 282 us
  matrix products  137 us (48%)
  blocking collectives  115 us (40%)
  local copies, waits for them, and re-layouts  15.9 us (6%)
  waiting for transfers between devices  4.86 us (2%)
  other arithmetic  4.29 us (2%)
  starting transfers between devices  4.22 us (1%)
    dot_general x17, matrix products, shift_sum(): jnp.einsum('ks,spw->kpw', weights, padded, precision=lax.Precision.HIGHES...  137 us
    all_to_all x1, blocking collectives, on_device(): lax.all_to_all(blocks, 'seg', split_axis=1, concat_axis=0, tiled=True)[:, 0]  109 us
    squeeze x1, local copies, waits for them, and re-layouts, on_device(): lax.all_to_all(blocks, 'seg', split_axis=1, concat_axis=0, tiled=True)[:, 0]  9.16 us
  transfers between devices with their start and end apart: 2, of which 2 were waited for; matrix products, arithmetic and copies ran while one was open for 0% of the time, Pallas kernels for 0%

commit v1 on v0

v1 whole, which is shorter than its diff:
```python
import functools

import jax
import jax.numpy as jnp
from jax import lax
from jax.experimental import pallas as pl
from jax.experimental.pallas import tpu as pltpu
from jax.sharding import PartitionSpec as P

HALO = 8
LANES = 128


def accumulate(side_ref, offsets_ref, maps_ref, fine_ref, msg_ref, edge_ref, data, weights, total, in_sems, out_sems):
    seg_count = offsets_ref.shape[1]
    spin_count = offsets_ref.shape[0]
    points = maps_ref.shape[0] // seg_count
    tiles = maps_ref.shape[1] // LANES
    rows = spin_count * points
    groups = spin_count // 8

    def fetch(tile):
        return pltpu.make_async_copy(
            maps_ref.at[:, pl.ds(tile * LANES, LANES)], data.at[tile], in_sems.at[tile]
        )

    for tile in range(tiles):
        fetch(tile).start()
    for index in range(2 * HALO + 1):
        hit = offsets_ref[...] == index - HALO
        weights[pl.ds(index * spin_count, spin_count), :] = jnp.where(hit, 1.0 / seg_count, 0.0).astype(jnp.bfloat16)
    total[...] = jnp.zeros_like(total)

    lane = lax.broadcasted_iota(jnp.int32, (spin_count, LANES), 1)

    for pair in range(tiles // 2):
        fetch(2 * pair).wait()
        fetch(2 * pair + 1).wait()

        def point_step(point, carry, pair=pair):
            block = jnp.concatenate(
                [data.at[2 * pair + half][pl.ds(point, seg_count, stride=points), :] for half in range(2)],
                axis=1,
            )
            high = block.astype(jnp.bfloat16)
            low = (block - high.astype(jnp.float32)).astype(jnp.bfloat16)
            taps = weights[...]
            product = jnp.dot(taps, high, preferred_element_type=jnp.float32) + jnp.dot(
                taps, low, preferred_element_type=jnp.float32
            )
            sums = [jnp.zeros((spin_count, LANES), jnp.float32) for _ in range(4)]
            for index in range(2 * HALO + 1):
                shift = index - HALO
                part = product[index * spin_count : (index + 1) * spin_count]
                left, right = part[:, :LANES], part[:, LANES:]
                if shift == 0:
                    sums[1] = sums[1] + left
                    sums[2] = sums[2] + right
                    continue
                left = pltpu.roll(left, (-shift) % LANES, 1)
                right = pltpu.roll(right, (-shift) % LANES, 1)
                if shift > 0:
                    same = lane < LANES - shift
                    sums[0] = sums[0] + jnp.where(same, 0.0, left)
                    sums[1] = sums[1] + jnp.where(same, left, right)
                    sums[2] = sums[2] + jnp.where(same, right, 0.0)
                else:
                    same = lane >= -shift
                    sums[1] = sums[1] + jnp.where(same, left, 0.0)
                    sums[2] = sums[2] + jnp.where(same, right, left)
                    sums[3] = sums[3] + jnp.where(same, 0.0, right)
            for place in range(4):
                target = total.at[2 * pair + place]
                for group in range(groups):
                    where = pl.ds(group * 8 * points + point, 8, stride=points)
                    target[where, :] = target[where, :] + sums[place][group * 8 : group * 8 + 8]
            return carry

        lax.fori_loop(0, points, point_step, 0)

    def emit(tile):
        return pltpu.make_async_copy(
            total.at[tile + 1], fine_ref.at[:, pl.ds(tile * LANES, LANES)], out_sems.at[tile]
        )

    for tile in range(1, tiles - 1):
        emit(tile).start()
    side = side_ref[0]
    low_side = side == 0
    row_lane = lax.broadcasted_iota(jnp.int32, (points, LANES), 1)
    outer = row_lane >= LANES - HALO
    inner = row_lane < HALO
    best = jnp.full((points, LANES), -jnp.inf, jnp.float32)
    for spin in range(spin_count):
        where = pl.ds(spin * points, points)
        for tile in range(1, tiles - 1):
            best = jnp.maximum(best, total[tile + 1, where, :])
        first, last = total[1, where, :], total[tiles, where, :]
        best = jnp.maximum(best, jnp.where(row_lane < HALO * side, -jnp.inf, first))
        best = jnp.maximum(best, jnp.where(row_lane >= LANES - HALO * (1 - side), -jnp.inf, last))
    msg_ref[pl.ds(groups * points, points), :] = best
    for group in range(groups):
        packed = jnp.zeros((points, LANES), jnp.float32)
        for slot in range(8):
            where = pl.ds((group * 8 + slot) * points, points)
            first, last = total[1, where, :], total[tiles, where, :]
            before, after = total[0, where, :], total[tiles + 1, where, :]
            mine = jnp.where(
                low_side, jnp.where(inner, after, last), jnp.where(inner, first, before)
            )
            mine = jnp.where(jnp.logical_or(inner, outer), mine, 0.0)
            packed = packed + pltpu.roll(mine, (HALO + 2 * HALO * slot) % LANES, 1)
        msg_ref[pl.ds(group * points, points), :] = packed
    edge_ref[...] = jnp.where(low_side, total[tiles], total[1])

    @pl.when(low_side)
    def _():
        emit(0).start()
        emit(0).wait()

    @pl.when(jnp.logical_not(low_side))
    def _():
        emit(tiles - 1).start()
        emit(tiles - 1).wait()

    for tile in range(1, tiles - 1):
        emit(tile).wait()


def finish(side_ref, mine_ref, theirs_ref, edge_ref, fine_in, fine_ref, peaks_ref, block, sem):
    points = peaks_ref.shape[1]
    groups = mine_ref.shape[0] // points - 1
    tiles = fine_ref.shape[1] // LANES
    side = side_ref[0]
    low_side = side == 0
    row_lane = lax.broadcasted_iota(jnp.int32, (points, LANES), 1)
    start = jnp.where(low_side, LANES - HALO, 0)
    edge = jnp.logical_and(row_lane >= start, row_lane < start + HALO)
    tail = pl.ds(groups * points, points)
    best = jnp.maximum(mine_ref[tail, :], theirs_ref[tail, :])
    for group in range(groups):
        where = pl.ds(group * points, points)
        packed = mine_ref[where, :] + theirs_ref[where, :]
        best = jnp.maximum(best, packed)
        for slot in range(8):
            rows = pl.ds((group * 8 + slot) * points, points)
            back = pltpu.roll(packed, (-(HALO + 2 * HALO * slot)) % LANES, 1)
            block[rows, :] = jnp.where(edge, back, edge_ref[rows, :])
    tile = jnp.where(low_side, tiles - 1, 0)
    copy = pltpu.make_async_copy(
        block, fine_ref.at[:, pl.ds(pl.multiple_of(tile * LANES, LANES), LANES)], sem
    )
    copy.start()
    top = jnp.max(best, axis=1, keepdims=True)
    row = lax.broadcasted_iota(jnp.int32, (points, LANES), 0)
    spread = jnp.max(jnp.where(row == row_lane, top, -jnp.inf), axis=0, keepdims=True)
    peaks_ref[...] = spread[:, :points]
    copy.wait()


def on_device(coarse, offsets):
    nseg = lax.axis_size("seg")
    side = lax.axis_index("freq").astype(jnp.int32).reshape(1)
    local_segs, points_all, bins = coarse.shape
    points = points_all // nseg
    segs = local_segs * nseg
    spins = offsets.shape[1]
    tiles = bins // LANES
    rows = spins * points
    groups = spins // 8
    blocks = coarse.reshape(local_segs, nseg, points, bins).transpose(1, 0, 2, 3)
    maps = lax.all_to_all(blocks, "seg", split_axis=0, concat_axis=0, tiled=True)
    smem = pl.BlockSpec(memory_space=pltpu.SMEM)
    vmem = pl.BlockSpec(memory_space=pltpu.VMEM)
    anywhere = pl.BlockSpec(memory_space=pl.ANY)
    fine, mine, edge = pl.pallas_call(
        accumulate,
        out_shape=(
            jax.ShapeDtypeStruct((rows, bins), jnp.float32),
            jax.ShapeDtypeStruct(((groups + 1) * points, LANES), jnp.float32),
            jax.ShapeDtypeStruct((rows, LANES), jnp.float32),
        ),
        in_specs=[smem, vmem, anywhere],
        out_specs=(anywhere, vmem, vmem),
        scratch_shapes=[
            pltpu.VMEM((tiles, segs * points, LANES), jnp.float32),
            pltpu.VMEM(((2 * HALO + 1) * spins, segs), jnp.bfloat16),
            pltpu.VMEM((tiles + 2, rows, LANES), jnp.float32),
            pltpu.SemaphoreType.DMA((tiles,)),
            pltpu.SemaphoreType.DMA((tiles,)),
        ],
        compiler_params=pltpu.CompilerParams(vmem_limit_bytes=40 * 1024 * 1024),
        name="accumulate",
    )(side, offsets.T, maps.reshape(segs * points, bins))
    theirs = lax.ppermute(mine, "freq", [(0, 1), (1, 0)])
    fine, peaks = pl.pallas_call(
        finish,
        out_shape=(
            jax.ShapeDtypeStruct((rows, bins), jnp.float32),
            jax.ShapeDtypeStruct((1, points), jnp.float32),
        ),
        in_specs=[smem, vmem, vmem, vmem, anywhere],
        out_specs=(anywhere, vmem),
        scratch_shapes=[pltpu.VMEM((rows, LANES), jnp.float32), pltpu.SemaphoreType.DMA],
        input_output_aliases={4: 0},
        name="finish",
    )(side, mine, theirs, edge, fine)
    return fine.reshape(spins, points, bins), peaks.reshape(points)


def solution(mesh):
    return jax.shard_map(
        on_device,
        mesh=mesh,
        in_specs=(P("seg", None, "freq"), P()),
        out_specs=(P(None, "seg", "freq"), P("seg")),
        check_vma=False,
    )
```

time: 285 us -> 155 us (0.54)
  the two profiles are of different devices: /device:TPU:0 before, /device:TPU:6 now
where the time goes in v1:
time: 155 us; the launch traced here: 154 us
  waiting for transfers between devices  113 us (73%)
  Pallas kernels  18.5 us (12%)
  starting transfers between devices  12.6 us (8%)
  local copies, waits for them, and re-layouts  9.54 us (6%)
    all_to_all x1, waiting for transfers between devices, on_device(): lax.all_to_all(blocks, 'seg', split_axis=0, concat_axis=0, tiled=True)  110 us
    pallas_call x1, Pallas kernels, on_device(): pl.pallas_call(accumulate, out_shape=(jax.ShapeDtypeStruct((rows, bins),...  16.3 us
    all_to_all x1, starting transfers between devices, on_device(): lax.all_to_all(blocks, 'seg', split_axis=0, concat_axis=0, tiled=True)  11.6 us
    transpose x1, local copies, waits for them, and re-layouts, on_device(): coarse.reshape(local_segs, nseg, points, bins).transpose(1, 0, 2, 3)  8.28 us
  transfers between devices with their start and end apart: 2, of which 2 were waited for; matrix products, arithmetic and copies ran while one was open for 0% of the time, Pallas kernels for 0%

profile of v1, /device:TPU:6, one launch (start us, length us, event | category | flops | bytes accessed | tf_op | source)
XLA Modules:
  0.0 154.5 jit_solution(3749507652033808638)
XLA Ops:
  0.6 8.3 %copy_bitcast_fusion = f32[64,4,8,1024]{3,2,1,0:T(8,128)} fusion(f32[4,512,1024]{2,1,0:T(8,128)} %param.2), kind=kLoop, calls=%fused_computation | loop fusion | bytes 16777216 | tf_op jit(solution)/shard_map/transpose | solution.py:171
  8.9 0.0 copy-start.1
  8.9 11.6 %all-to-all-start = ((f32[64,4,8,1024]{3,2,1,0:T(8,128)}), f32[64,4,8,1024]{3,2,1,0:T(8,128)}, u32[]{:S(2)}, u32[]{:S(2)}) async-start(f32[64,4,8,1024]{3,2,1,0:T(8,128)} %copy_bitcast_fusion), calls=%async_computation | async-start | bytes 16777216 | tf_op jit(solution)/shard_map/all_to_all | solution.py:172
  20.5 110.4 %all-to-all-done = f32[64,4,8,1024]{3,2,1,0:T(8,128)} async-done(((f32[64,4,8,1024]{3,2,1,0:T(8,128)}), f32[64,4,8,1024]{3,2,1,0:T(8,128)}, u32[]{:S(2)}, u32[]{:S(2)}) %all-to-all-start) | async-done | bytes 8388640 | tf_op jit(solution)/shard_map/all_to_all | solution.py:172
  130.9 0.0 copy-done.1
  130.9 16.3 %accumulate.1 = (f32[256,1024]{1,0:T(8,128)}, f32[40,128]{1,0:T(8,128)S(1)}, f32[256,128]{1,0:T(8,128)S(1)}) custom-call(s32[1]{0:T(128)} %bitcast.side_ref, s32[32,256]{1,0:T(8,128)S(1)} %bitcast.10, f32[2048,1024]{1,0:T(8,128)} %bitcast.4.maps_ref), custom_call_target="tpu_custom_call" | custom-call | tf_op jit(solution)/shard_map/accumulate/pallas_call | solution.py:176
  147.2 0.0 copy-start
  147.2 0.6 copy-done
  147.9 0.0 copy-start.2
  147.9 1.0 collective-permute-start
  148.9 2.8 %collective-permute-done.theirs_ref = f32[40,128]{1,0:T(8,128)S(1)} collective-permute-done((f32[40,128]{1,0:T(8,128)S(1)}, f32[40,128]{1,0:T(8,128)S(1)}, u32[]{:S(2)}, u32[]{:S(2)}) %collective-permute-start) | collective-permute-done | bytes 20512 | tf_op jit(solution)/shard_map/ppermute | solution.py:195
  151.6 0.0 copy-start.3
  151.6 0.0 copy-done.2
  151.6 0.6 copy-done.3
  152.2 2.2 %finish.1 = (f32[256,1024]{1,0:T(8,128)}, f32[1,8]{1,0:T(1,128)}) custom-call(s32[1]{0:T(128)} %bitcast.side_ref, f32[40,128]{1,0:T(8,128)} %copy-done.2, f32[40,128]{1,0:T(8,128)} %copy-done.3, f32[256,128]{1,0:T(8,128)} %copy-done, f32[256,1024]{1,0:T(8,128)} %get-tuple-element.9.fine_in), custom_call_target="tpu_custom_call", output_to_operand_aliasing={{0}: (4, {})} | custom-call | tf_op jit(solution)/shard_map/finish/pallas_call | solution.py:196
Async XLA Ops:
  8.9 122.0 %copy-start.1 = (s32[256,32]{0,1:T(8,128)S(1)}, s32[256,32]{0,1:T(8,128)}, u32[]{:S(2)}) copy-start(s32[256,32]{0,1:T(8,128)} %param.3) | copy-start | bytes 98308
  8.9 122.0 %all-to-all-start = ((f32[64,4,8,1024]{3,2,1,0:T(8,128)}), f32[64,4,8,1024]{3,2,1,0:T(8,128)}, u32[]{:S(2)}, u32[]{:S(2)}) async-start(f32[64,4,8,1024]{3,2,1,0:T(8,128)} %copy_bitcast_fusion), calls=%async_computation | async-start | bytes 16777216 | tf_op jit(solution)/shard_map/all_to_all | solution.py:172
  147.2 0.7 copy-start
  147.9 3.8 %copy-start.2 = (f32[40,128]{1,0:T(8,128)}, f32[40,128]{1,0:T(8,128)S(1)}, u32[]{:S(2)}) copy-start(f32[40,128]{1,0:T(8,128)S(1)} %get-tuple-element.7.mine_ref) | copy-start | bytes 61444
  147.9 3.8 %collective-permute-start = (f32[40,128]{1,0:T(8,128)S(1)}, f32[40,128]{1,0:T(8,128)S(1)}, u32[]{:S(2)}, u32[]{:S(2)}) collective-permute-start(f32[40,128]{1,0:T(8,128)S(1)} %get-tuple-element.7.mine_ref), channel_id=1, source_target_pairs={{0,1},{1,0},{2,3},{3,2},{4,5},{5,4},{6,7},{7,6},{8,9},{9,8},{10,11... | collective-permute-start | bytes 61448 | tf_op jit(solution)/shard_map/ppermute | solution.py:195
  151.6 0.6 copy-start.3

commit v2 on v1

v2 whole, which is shorter than its diff:
```python
import jax
import jax.numpy as jnp
from jax import lax
from jax.experimental import pallas as pl
from jax.experimental.pallas import tpu as pltpu
from jax.sharding import PartitionSpec as P

HALO = 8
LANES = 128
SHIFTS = 2 * HALO + 1
OUTER, MIDDLE = 4, 2


def exchange_order(count):
    inner = count // (OUTER * MIDDLE)
    return [
        (outer * MIDDLE + middle) * inner + place
        for outer in range(OUTER)
        for place in range(inner)
        for middle in range(MIDDLE)
    ]


def pack(offsets_ref, coarse_ref, blocks_ref, taps_ref, sems):
    local, outer, middle, inner = coarse_ref.shape[:4]
    spin_count, seg_count = offsets_ref.shape
    copies = [
        pltpu.make_async_copy(coarse_ref.at[s, :, m], blocks_ref.at[:, :, m, s], sems.at[s, m])
        for s in range(local)
        for m in range(middle)
    ]
    for copy in copies:
        copy.start()
    source = lax.broadcasted_iota(jnp.int32, (seg_count, seg_count), 0)
    arrival = lax.broadcasted_iota(jnp.int32, (seg_count, seg_count), 1)
    device, s = arrival // local, arrival % local
    m, rest = device % middle, device // middle
    natural = (((rest // inner) * middle + m) * inner + rest % inner) * local + s
    move = jnp.where(source == natural, 1.0, 0.0).astype(jnp.bfloat16)
    arrived = jnp.dot(
        offsets_ref[...].astype(jnp.float32).astype(jnp.bfloat16), move, preferred_element_type=jnp.float32
    )
    for index in range(SHIFTS):
        hit = arrived == float(index - HALO)
        taps_ref[pl.ds(index * spin_count, spin_count), :] = jnp.where(hit, 1.0 / seg_count, 0.0).astype(jnp.bfloat16)
    for copy in copies:
        copy.wait()


def accumulate(taps_ref, maps_ref, fine_ref, msg_ref, rest_ref, data, total, in_sems, out_sems):
    seg_count = taps_ref.shape[1]
    spin_count = taps_ref.shape[0] // SHIFTS
    points = maps_ref.shape[0] // seg_count
    tiles = maps_ref.shape[1] // LANES
    pairs = tiles // 2
    groups = spin_count // 8

    def fetch(tile):
        return pltpu.make_async_copy(
            maps_ref.at[:, pl.ds(tile * LANES, LANES)], data.at[tile], in_sems.at[tile]
        )

    def emit(tile):
        return pltpu.make_async_copy(
            total.at[tile + 1], fine_ref.at[:, pl.ds(tile * LANES, LANES)], out_sems.at[tile]
        )

    for tile in range(4):
        fetch(tile).start()
    total[...] = jnp.zeros_like(total)
    lane = lax.broadcasted_iota(jnp.int32, (spin_count, LANES), 1)

    for pair in range(pairs):
        fetch(2 * pair).wait()
        fetch(2 * pair + 1).wait()
        if pair + 2 < pairs:
            fetch(2 * pair + 4).start()
            fetch(2 * pair + 5).start()

        def point_step(point, carry, pair=pair):
            block = jnp.concatenate(
                [data.at[2 * pair + half][pl.ds(point, seg_count, stride=points), :] for half in range(2)],
                axis=1,
            )
            high = block.astype(jnp.bfloat16)
            low = (block - high.astype(jnp.float32)).astype(jnp.bfloat16)
            taps = taps_ref[...]
            product = jnp.dot(taps, high, preferred_element_type=jnp.float32) + jnp.dot(
                taps, low, preferred_element_type=jnp.float32
            )
            sums = [jnp.zeros((spin_count, LANES), jnp.float32) for _ in range(4)]
            for index in range(SHIFTS):
                shift = index - HALO
                part = product[index * spin_count : (index + 1) * spin_count]
                left, right = part[:, :LANES], part[:, LANES:]
                if shift == 0:
                    sums[1] = sums[1] + left
                    sums[2] = sums[2] + right
                    continue
                left = pltpu.roll(left, (-shift) % LANES, 1)
                right = pltpu.roll(right, (-shift) % LANES, 1)
                if shift > 0:
                    same = lane < LANES - shift
                    sums[0] = sums[0] + jnp.where(same, 0.0, left)
                    sums[1] = sums[1] + jnp.where(same, left, right)
                    sums[2] = sums[2] + jnp.where(same, right, 0.0)
                else:
                    same = lane >= -shift
                    sums[1] = sums[1] + jnp.where(same, left, 0.0)
                    sums[2] = sums[2] + jnp.where(same, right, left)
                    sums[3] = sums[3] + jnp.where(same, 0.0, right)
            for place in range(4):
                target = total.at[2 * pair + place]
                for group in range(groups):
                    where = pl.ds(group * 8 * points + point, 8, stride=points)
                    target[where, :] = target[where, :] + sums[place][group * 8 : group * 8 + 8]
            return carry

        lax.fori_loop(0, points, point_step, 0, unroll=4)
        if pair + 1 < pairs:
            for tile in range(max(1, 2 * pair - 1), 2 * pair + 1):
                emit(tile).start()

    side = lax.axis_index("freq")
    low_side = side == 0
    row_lane = lax.broadcasted_iota(jnp.int32, (points, LANES), 1)
    outer = row_lane >= LANES - HALO
    inner = row_lane < HALO
    best = jnp.full((points, LANES), -jnp.inf, jnp.float32)
    for spin in range(spin_count):
        where = pl.ds(spin * points, points)
        for tile in range(1, tiles - 1):
            best = jnp.maximum(best, total[tile + 1, where, :])
        first, last = total[1, where, :], total[tiles, where, :]
        best = jnp.maximum(best, jnp.where(row_lane < HALO * side, -jnp.inf, first))
        best = jnp.maximum(best, jnp.where(row_lane >= LANES - HALO * (1 - side), -jnp.inf, last))
    msg_ref[pl.ds(groups * points, points), :] = best
    for group in range(groups):
        packed = jnp.zeros((points, LANES), jnp.float32)
        for slot in range(8):
            where = pl.ds((group * 8 + slot) * points, points)
            first, last = total[1, where, :], total[tiles, where, :]
            before, after = total[0, where, :], total[tiles + 1, where, :]
            mine = jnp.where(
                low_side, jnp.where(inner, after, last), jnp.where(inner, first, before)
            )
            mine = jnp.where(jnp.logical_or(inner, outer), mine, 0.0)
            packed = packed + pltpu.roll(mine, (HALO + 2 * HALO * slot) % LANES, 1)
        msg_ref[pl.ds(group * points, points), :] = packed
    rest_ref[0] = total[1]
    for place in range(3):
        rest_ref[1 + place] = total[tiles - 2 + place]
    for tile in range(1, tiles - 3):
        emit(tile).wait()


def finish(mine_ref, theirs_ref, rest_ref, fine_in, fine_ref, peaks_ref, first, last, sems):
    points = peaks_ref.shape[1]
    groups = mine_ref.shape[0] // points - 1
    tiles = fine_ref.shape[1] // LANES

    def emit(source, tile, place):
        return pltpu.make_async_copy(source, fine_ref.at[:, pl.ds(tile * LANES, LANES)], sems.at[place])

    copies = [
        emit(first, 0, 0),
        emit(rest_ref.at[1], tiles - 3, 1),
        emit(rest_ref.at[2], tiles - 2, 2),
        emit(last, tiles - 1, 3),
    ]
    copies[1].start()
    copies[2].start()
    side = lax.axis_index("freq")
    row_lane = lax.broadcasted_iota(jnp.int32, (points, LANES), 1)
    tail = pl.ds(groups * points, points)
    best = jnp.maximum(mine_ref[tail, :], theirs_ref[tail, :])
    for group in range(groups):
        where = pl.ds(group * points, points)
        packed = mine_ref[where, :] + theirs_ref[where, :]
        best = jnp.maximum(best, packed)
        for slot in range(8):
            rows = pl.ds((group * 8 + slot) * points, points)
            back = pltpu.roll(packed, (-(HALO + 2 * HALO * slot)) % LANES, 1)
            first[rows, :] = jnp.where(row_lane < HALO * side, back, rest_ref[0, rows, :])
            last[rows, :] = jnp.where(row_lane >= LANES - HALO * (1 - side), back, rest_ref[3, rows, :])
    copies[0].start()
    copies[3].start()
    top = jnp.max(best, axis=1, keepdims=True)
    row = lax.broadcasted_iota(jnp.int32, (points, LANES), 0)
    spread = jnp.max(jnp.where(row == row_lane, top, -jnp.inf), axis=0, keepdims=True)
    peaks_ref[...] = spread[:, :points]
    for copy in copies:
        copy.wait()


def on_device(coarse, offsets):
    nseg = lax.axis_size("seg")
    local_segs, points_all, bins = coarse.shape
    points = points_all // nseg
    segs = local_segs * nseg
    spins = offsets.shape[1]
    tiles = bins // LANES
    rows = spins * points
    groups = spins // 8
    inner = nseg // (OUTER * MIDDLE)
    vmem = pl.BlockSpec(memory_space=pltpu.VMEM)
    anywhere = pl.BlockSpec(memory_space=pl.ANY)
    mib = 1024 * 1024
    blocks, taps = pl.pallas_call(
        pack,
        out_shape=(
            jax.ShapeDtypeStruct((OUTER, inner, MIDDLE, local_segs, points, bins), jnp.float32),
            jax.ShapeDtypeStruct((SHIFTS * spins, segs), jnp.bfloat16),
        ),
        in_specs=[vmem, pl.BlockSpec(memory_space=pltpu.HBM)],
        out_specs=(vmem, vmem),
        scratch_shapes=[pltpu.SemaphoreType.DMA((local_segs, MIDDLE))],
        compiler_params=pltpu.CompilerParams(vmem_limit_bytes=16 * mib),
        name="pack",
    )(offsets.T, coarse.reshape(local_segs, OUTER, MIDDLE, inner, points, bins))
    maps = lax.all_to_all(
        blocks.reshape(nseg, local_segs, points, bins),
        "seg",
        split_axis=0,
        concat_axis=0,
        tiled=True,
        axis_index_groups=[exchange_order(nseg)],
    )
    fine, mine, rest = pl.pallas_call(
        accumulate,
        out_shape=(
            jax.ShapeDtypeStruct((rows, bins), jnp.float32),
            jax.ShapeDtypeStruct(((groups + 1) * points, LANES), jnp.float32),
            jax.ShapeDtypeStruct((4, rows, LANES), jnp.float32),
        ),
        in_specs=[vmem, anywhere],
        out_specs=(anywhere, vmem, vmem),
        scratch_shapes=[
            pltpu.VMEM((tiles, segs * points, LANES), jnp.float32),
            pltpu.VMEM((tiles + 2, rows, LANES), jnp.float32),
            pltpu.SemaphoreType.DMA((tiles,)),
            pltpu.SemaphoreType.DMA((tiles,)),
        ],
        compiler_params=pltpu.CompilerParams(vmem_limit_bytes=24 * mib),
        name="accumulate",
    )(taps, maps.reshape(segs * points, bins))
    theirs = lax.ppermute(mine, "freq", [(0, 1), (1, 0)])
    fine, peaks = pl.pallas_call(
        finish,
        out_shape=(
            jax.ShapeDtypeStruct((rows, bins), jnp.float32),
            jax.ShapeDtypeStruct((1, points), jnp.float32),
        ),
        in_specs=[vmem, vmem, vmem, anywhere],
        out_specs=(anywhere, vmem),
        scratch_shapes=[
            pltpu.VMEM((rows, LANES), jnp.float32),
            pltpu.VMEM((rows, LANES), jnp.float32),
            pltpu.SemaphoreType.DMA((4,)),
        ],
        input_output_aliases={3: 0},
        compiler_params=pltpu.CompilerParams(vmem_limit_bytes=4 * mib),
        name="finish",
    )(mine, theirs, rest, fine)
    return fine.reshape(spins, points, bins), peaks.reshape(points)


def solution(mesh):
    return jax.shard_map(
        on_device,
        mesh=mesh,
        in_specs=(P("seg", None, "freq"), P()),
        out_specs=(P(None, "seg", "freq"), P("seg")),
        check_vma=False,
    )
```

time: 155 us -> 130 us (0.84)
  the two profiles are of different devices: /device:TPU:6 before, /device:TPU:0 now
where the time goes in v2:
time: 130 us
  blocking collectives  109 us (84%)
  Pallas kernels  12.2 us (9%)
  local copies, waits for them, and re-layouts  4.13 us (3%)
  waiting for transfers between devices  2.77 us (2%)
    all_to_all x1, blocking collectives, on_device(): lax.all_to_all(blocks.reshape(nseg, local_segs, points, bins), 'seg', spl...  109 us
    pallas_call x1, Pallas kernels, on_device(): pl.pallas_call(accumulate, out_shape=(jax.ShapeDtypeStruct((rows, bins),...  9.94 us
    unnamed x4, local copies, waits for them, and re-layouts  4.13 us
    ppermute x1, waiting for transfers between devices, on_device(): theirs = lax.ppermute(mine, 'freq', [(0, 1), (1, 0)])  2.77 us
  transfers between devices with their start and end apart: 1, of which 1 were waited for; matrix products, arithmetic and copies ran while one was open for 0% of the time, Pallas kernels for 0%

profile of v2, /device:TPU:0, one launch (start us, length us, event | category | flops | bytes accessed | tf_op | source)
XLA Modules:
  0.0 130.1 jit_solution(2833828623729083666)
XLA Ops:
  0.6 0.0 copy-start
  0.6 3.4 %copy-done = f32[4,512,1024]{2,1,0:T(8,128)S(1)} copy-done((f32[4,512,1024]{2,1,0:T(8,128)S(1)}, f32[4,512,1024]{2,1,0:T(8,128)}, u32[]{:S(2)}) %copy-start) | copy-done | bytes 8388632
  4.0 0.0 copy-start.1
  4.0 0.8 copy-done.1
  4.8 0.9 pack.1
  5.6 109.3 %all_to_all.5 = f32[64,4,8,1024]{3,2,1,0:T(8,128)S(1)} all-to-all(f32[64,4,8,1024]{3,2,1,0:T(8,128)S(1)} %bitcast.8), channel_id=1, replica_groups={{0,16,2,18,4,20,6,22,8,24,10,26,12,28,14,30,32,48,34,50,36,52,38,54,40,..., dimensions={0} | all-to-all | bytes 16777216 | tf_op jit(solution)/shard_map/all_to_all | solution.py:221
  114.9 9.9 %accumulate.1 = (f32[256,1024]{1,0:T(8,128)}, f32[40,128]{1,0:T(8,128)S(1)}, f32[4,256,128]{2,1,0:T(8,128)S(1)}) custom-call(bf16[544,256]{1,0:T(8,128)(2,1)S(1)} %get-tuple-element.9.taps_ref, f32[2048,1024]{1,0:T(8,128)S(1)} %bitcast.6), custom_call_target="tpu_custom_call" | custom-call | tf_op jit(solution)/shard_map/accumulate/pallas_call | solution.py:229
  124.9 1.1 collective-permute-start
  126.0 2.8 %collective-permute-done.theirs_ref = f32[40,128]{1,0:T(8,128)S(1)} collective-permute-done((f32[40,128]{1,0:T(8,128)S(1)}, f32[40,128]{1,0:T(8,128)S(1)}, u32[]{:S(2)}, u32[]{:S(2)}) %collective-permute-start) | collective-permute-done | bytes 20512 | tf_op jit(solution)/shard_map/ppermute | solution.py:247
  128.8 1.4 %finish.1 = (f32[256,1024]{1,0:T(8,128)}, f32[1,8]{1,0:T(1,128)}) custom-call(f32[40,128]{1,0:T(8,128)S(1)} %get-tuple-element.11.mine_ref, f32[40,128]{1,0:T(8,128)S(1)} %collective-permute-done.theirs_ref, f32[4,256,128]{2,1,0:T(8,128)S(1)} %get-tuple-element.12.rest_ref, f32[256,1024]{1,0:T(8,128)} %get-tuple-element.13.fine_in), custom_call_target="tpu_custom_call", output_to_operand_aliasing={{0}: (3, {})} | custom-call | tf_op jit(solution)/shard_map/finish/pallas_call | solution.py:248
Async XLA Ops:
  0.6 3.4 %copy-start = (f32[4,512,1024]{2,1,0:T(8,128)S(1)}, f32[4,512,1024]{2,1,0:T(8,128)}, u32[]{:S(2)}) copy-start(f32[4,512,1024]{2,1,0:T(8,128)} %param.2) | copy-start | bytes 25165828
  4.0 0.8 copy-start.1
  124.9 3.9 %collective-permute-start = (f32[40,128]{1,0:T(8,128)S(1)}, f32[40,128]{1,0:T(8,128)S(1)}, u32[]{:S(2)}, u32[]{:S(2)}) collective-permute-start(f32[40,128]{1,0:T(8,128)S(1)} %get-tuple-element.11.mine_ref), channel_id=1, source_target_pairs={{0,1},{1,0},{2,3},{3,2},{4,5},{5,4},{6,7},{7,6},{8,9},{9,8},{10,11... | collective-permute-start | bytes 61448 | tf_op jit(solution)/shard_map/ppermute | solution.py:247

commit v3 on v2

--- a/solution.py
+++ b/solution.py
@@ -1,3 +1,5 @@
+import functools
+
 import jax
 import jax.numpy as jnp
 from jax import lax
@@ -21,9 +23,8 @@
     ]
 
 
-def pack(offsets_ref, coarse_ref, blocks_ref, taps_ref, sems):
+def pack(coarse_ref, blocks_ref, sems):
     local, outer, middle, inner = coarse_ref.shape[:4]
-    spin_count, seg_count = offsets_ref.shape
     copies = [
         pltpu.make_async_copy(coarse_ref.at[s, :, m], blocks_ref.at[:, :, m, s], sems.at[s, m])
         for s in range(local)
@@ -31,6 +32,13 @@
     ]
     for copy in copies:
         copy.start()
+    for copy in copies:
+        copy.wait()
+
+
+def write_taps(local, offsets_ref, taps_ref):
+    spin_count, seg_count = offsets_ref.shape
+    middle, inner = MIDDLE, seg_count // local // (OUTER * MIDDLE)
     source = lax.broadcasted_iota(jnp.int32, (seg_count, seg_count), 0)
     arrival = lax.broadcasted_iota(jnp.int32, (seg_count, seg_count), 1)
     device, s = arrival // local, arrival % local
@@ -43,13 +51,10 @@
     for index in range(SHIFTS):
         hit = arrived == float(index - HALO)
         taps_ref[pl.ds(index * spin_count, spin_count), :] = jnp.where(hit, 1.0 / seg_count, 0.0).astype(jnp.bfloat16)
-    for copy in copies:
-        copy.wait()
-
-
-def accumulate(taps_ref, maps_ref, fine_ref, msg_ref, rest_ref, data, total, in_sems, out_sems):
-    seg_count = taps_ref.shape[1]
-    spin_count = taps_ref.shape[0] // SHIFTS
+
+
+def accumulate(local, offsets_ref, maps_ref, fine_ref, msg_ref, rest_ref, data, taps_ref, total, early, late, in_sems, out_sems):
+    spin_count, seg_count = offsets_ref.shape
     points = maps_ref.shape[0] // seg_count
     tiles = maps_ref.shape[1] // LANES
     pairs = tiles // 2
@@ -67,56 +72,71 @@
 
     for tile in range(4):
         fetch(tile).start()
+    write_taps(local, offsets_ref, taps_ref)
     total[...] = jnp.zeros_like(total)
     lane = lax.broadcasted_iota(jnp.int32, (spin_count, LANES), 1)
 
-    for pair in range(pairs):
+    def multiply(pair, point, product):
+        block = jnp.concatenate(
+            [data.at[2 * pair + half][pl.ds(point, seg_count, stride=points), :] for half in range(2)],
+            axis=1,
+        )
+        high = block.astype(jnp.bfloat16)
+        low = (block - high.astype(jnp.float32)).astype(jnp.bfloat16)
+        taps = taps_ref[...]
+        product[...] = jnp.dot(taps, high, preferred_element_type=jnp.float32) + jnp.dot(
+            taps, low, preferred_element_type=jnp.float32
+        )
+
+    def combine(pair, point, product):
+        sums = [jnp.zeros((spin_count, LANES), jnp.float32) for _ in range(4)]
+        for index in range(SHIFTS):
+            shift = index - HALO
+            where = pl.ds(index * spin_count, spin_count)
+            left, right = product[where, :LANES], product[where, LANES:]
+            if shift == 0:
+                sums[1] = sums[1] + left
+                sums[2] = sums[2] + right
+                continue
+            left = pltpu.roll(left, (-shift) % LANES, 1)
+            right = pltpu.roll(right, (-shift) % LANES, 1)
+            if shift > 0:
+                same = lane < LANES - shift
+                sums[0] = sums[0] + jnp.where(same, 0.0, left)
+                sums[1] = sums[1] + jnp.where(same, left, right)
+                sums[2] = sums[2] + jnp.where(same, right, 0.0)
+            else:
+                same = lane >= -shift
+                sums[1] = sums[1] + jnp.where(same, left, 0.0)
+                sums[2] = sums[2] + jnp.where(same, right, left)
+                sums[3] = sums[3] + jnp.where(same, 0.0, right)
+        for place in range(4):
+            target = total.at[2 * pair + place]
+            for group in range(groups):
+                where = pl.ds(group * 8 * points + point, 8, stride=points)
+                target[where, :] = target[where, :] + sums[place][group * 8 : group * 8 + 8]
+
+    def arrive(pair):
         fetch(2 * pair).wait()
         fetch(2 * pair + 1).wait()
         if pair + 2 < pairs:
             fetch(2 * pair + 4).start()
             fetch(2 * pair + 5).start()
 
-        def point_step(point, carry, pair=pair):
-            block = jnp.concatenate(
-                [data.at[2 * pair + half][pl.ds(point, seg_count, stride=points), :] for half in range(2)],
-                axis=1,
-            )
-            high = block.astype(jnp.bfloat16)
-            low = (block - high.astype(jnp.float32)).astype(jnp.bfloat16)
-            taps = taps_ref[...]
-            product = jnp.dot(taps, high, preferred_element_type=jnp.float32) + jnp.dot(
-                taps, low, preferred_element_type=jnp.float32
-            )
-            sums = [jnp.zeros((spin_count, LANES), jnp.float32) for _ in range(4)]
-            for index in range(SHIFTS):
-                shift = index - HALO
-                part = product[index * spin_count : (index + 1) * spin_count]
-                left, right = part[:, :LANES], part[:, LANES:]
-                if shift == 0:
-                    sums[1] = sums[1] + left
-                    sums[2] = sums[2] + right
-                    continue
-                left = pltpu.roll(left, (-shift) % LANES, 1)
-                right = pltpu.roll(right, (-shift) % LANES, 1)
-                if shift > 0:
-                    same = lane < LANES - shift
-                    sums[0] = sums[0] + jnp.where(same, 0.0, left)
-                    sums[1] = sums[1] + jnp.where(same, left, right)
-                    sums[2] = sums[2] + jnp.where(same, right, 0.0)
-                else:
-                    same = lane >= -shift
-                    sums[1] = sums[1] + jnp.where(same, left, 0.0)
-                    sums[2] = sums[2] + jnp.where(same, right, left)
-                    sums[3] = sums[3] + jnp.where(same, 0.0, right)
-            for place in range(4):
-                target = total.at[2 * pair + place]
-                for group in range(groups):
-                    where = pl.ds(group * 8 * points + point, 8, stride=points)
-                    target[where, :] = target[where, :] + sums[place][group * 8 : group * 8 + 8]
-            return carry
-
-        lax.fori_loop(0, points, point_step, 0, unroll=4)
+    half = points // 2
+    arrive(0)
+    for point in range(half):
+        multiply(0, point, early.at[point])
+    for pair in range(pairs):
+        if pair + 1 < pairs:
+            arrive(pair + 1)
+        for point in range(half):
+            multiply(pair, half + point, late.at[point])
+            combine(pair, point, early.at[point])
+        for point in range(half):
+            if pair + 1 < pairs:
+                multiply(pair + 1, point, early.at[point])
+            combine(pair, half + point, late.at[point])
         if pair + 1 < pairs:
             for tile in range(max(1, 2 * pair - 1), 2 * pair + 1):
                 emit(tile).start()
@@ -206,18 +226,15 @@
     vmem = pl.BlockSpec(memory_space=pltpu.VMEM)
     anywhere = pl.BlockSpec(memory_space=pl.ANY)
     mib = 1024 * 1024
-    blocks, taps = pl.pallas_call(
+    blocks = pl.pallas_call(
         pack,
-        out_shape=(
-            jax.ShapeDtypeStruct((OUTER, inner, MIDDLE, local_segs, points, bins), jnp.float32),
-            jax.ShapeDtypeStruct((SHIFTS * spins, segs), jnp.bfloat16),
-        ),
-        in_specs=[vmem, pl.BlockSpec(memory_space=pltpu.HBM)],
-        out_specs=(vmem, vmem),
+        out_shape=jax.ShapeDtypeStruct((OUTER, inner, MIDDLE, local_segs, points, bins), jnp.float32),
+        in_specs=[anywhere],
+        out_specs=vmem,
         scratch_shapes=[pltpu.SemaphoreType.DMA((local_segs, MIDDLE))],
-        compiler_params=pltpu.CompilerParams(vmem_limit_bytes=16 * mib),
+        compiler_params=pltpu.CompilerParams(vmem_limit_bytes=44 * mib),
         name="pack",
-    )(offsets.T, coarse.reshape(local_segs, OUTER, MIDDLE, inner, points, bins))
+    )(coarse.reshape(local_segs, OUTER, MIDDLE, inner, points, bins))
     maps = lax.all_to_all(
         blocks.reshape(nseg, local_segs, points, bins),
         "seg",
@@ -227,7 +244,7 @@
         axis_index_groups=[exchange_order(nseg)],
     )
     fine, mine, rest = pl.pallas_call(
-        accumulate,
+        functools.partial(accumulate, local_segs),
         out_shape=(
             jax.ShapeDtypeStruct((rows, bins), jnp.float32),
             jax.ShapeDtypeStruct(((groups + 1) * points, LANES), jnp.float32),
@@ -237,13 +254,16 @@
         out_specs=(anywhere, vmem, vmem),
         scratch_shapes=[
             pltpu.VMEM((tiles, segs * points, LANES), jnp.float32),
+            pltpu.VMEM((SHIFTS * spins, segs), jnp.bfloat16),
             pltpu.VMEM((tiles + 2, rows, LANES), jnp.float32),
+            pltpu.VMEM((points // 2, SHIFTS * spins, 2 * LANES), jnp.float32),
+            pltpu.VMEM((points // 2, SHIFTS * spins, 2 * LANES), jnp.float32),
             pltpu.SemaphoreType.DMA((tiles,)),
             pltpu.SemaphoreType.DMA((tiles,)),
         ],
         compiler_params=pltpu.CompilerParams(vmem_limit_bytes=24 * mib),
         name="accumulate",
-    )(taps, maps.reshape(segs * points, bins))
+    )(offsets.T, maps.reshape(segs * points, bins))
     theirs = lax.ppermute(mine, "freq", [(0, 1), (1, 0)])
     fine, peaks = pl.pallas_call(
         finish,

time: 130 us -> 127 us (0.977)
  local copies, waits for them, and re-layouts: 4.13 us -> 0.01 us
    unnamed x4 -> x2, local copies, waits for them, and re-layouts: 4.13 us -> 0.01 us
where the time goes in v3:
time: 127 us
  blocking collectives  109 us (86%)
  Pallas kernels  13.1 us (10%)
  waiting for transfers between devices  2.75 us (2%)
    all_to_all x1, blocking collectives, on_device(): lax.all_to_all(blocks.reshape(nseg, local_segs, points, bins), 'seg', spl...  109 us
    pallas_call x1, Pallas kernels, on_device(): pl.pallas_call(functools.partial(accumulate, local_segs), out_shape=(jax....  8.3 us
    pallas_call x1, Pallas kernels, on_device(): pl.pallas_call(pack, out_shape=jax.ShapeDtypeStruct((OUTER, inner, MIDDLE...  3.49 us
    ppermute x1, waiting for transfers between devices, on_device(): theirs = lax.ppermute(mine, 'freq', [(0, 1), (1, 0)])  2.75 us
  transfers between devices with their start and end apart: 1, of which 1 were waited for; matrix products, arithmetic and copies ran while one was open for 0% of the time, Pallas kernels for 0%

profile of v3, /device:TPU:0, one launch (start us, length us, event | category | flops | bytes accessed | tf_op | source)
XLA Modules:
  0.0 127.0 jit_solution(17746200163331505129)
XLA Ops:
  0.6 3.5 %pack.1 = f32[4,8,2,4,8,1024]{5,4,3,2,1,0:T(8,128)S(1)} custom-call(f32[4,4,2,8,8,1024]{5,4,3,2,1,0:T(8,128)} %bitcast.9), custom_call_target="tpu_custom_call" | custom-call | tf_op jit(solution)/shard_map/pack/pallas_call | solution.py:229
  4.1 0.0 copy-start
  4.1 109.3 %all_to_all.5 = f32[64,4,8,1024]{3,2,1,0:T(8,128)S(1)} all-to-all(f32[64,4,8,1024]{3,2,1,0:T(8,128)S(1)} %bitcast.7), channel_id=1, replica_groups={{0,16,2,18,4,20,6,22,8,24,10,26,12,28,14,30,32,48,34,50,36,52,38,54,40,..., dimensions={0} | all-to-all | bytes 16777216 | tf_op jit(solution)/shard_map/all_to_all | solution.py:238
  113.4 0.0 copy-done
  113.4 8.3 %accumulate.1 = (f32[256,1024]{1,0:T(8,128)}, f32[40,128]{1,0:T(8,128)S(1)}, f32[4,256,128]{2,1,0:T(8,128)S(1)}) custom-call(s32[32,256]{1,0:T(8,128)S(1)} %bitcast.8, f32[2048,1024]{1,0:T(8,128)S(1)} %bitcast.6), custom_call_target="tpu_custom_call" | custom-call | tf_op jit(solution)/shard_map/accumulate/pallas_call | solution.py:246
  121.7 1.1 collective-permute-start
  122.8 2.8 %collective-permute-done.theirs_ref = f32[40,128]{1,0:T(8,128)S(1)} collective-permute-done((f32[40,128]{1,0:T(8,128)S(1)}, f32[40,128]{1,0:T(8,128)S(1)}, u32[]{:S(2)}, u32[]{:S(2)}) %collective-permute-start) | collective-permute-done | bytes 20512 | tf_op jit(solution)/shard_map/ppermute | solution.py:267
  125.6 1.4 %finish.1 = (f32[256,1024]{1,0:T(8,128)}, f32[1,8]{1,0:T(1,128)}) custom-call(f32[40,128]{1,0:T(8,128)S(1)} %get-tuple-element.7.mine_ref, f32[40,128]{1,0:T(8,128)S(1)} %collective-permute-done.theirs_ref, f32[4,256,128]{2,1,0:T(8,128)S(1)} %get-tuple-element.8.rest_ref, f32[256,1024]{1,0:T(8,128)} %get-tuple-element.9.fine_in), custom_call_target="tpu_custom_call", output_to_operand_aliasing={{0}: (3, {})} | custom-call | tf_op jit(solution)/shard_map/finish/pallas_call | solution.py:268
Async XLA Ops:
  4.1 109.3 %copy-start = (s32[256,32]{0,1:T(8,128)S(1)}, s32[256,32]{0,1:T(8,128)}, u32[]{:S(2)}) copy-start(s32[256,32]{0,1:T(8,128)} %param.3) | copy-start | bytes 98308
  121.7 3.9 %collective-permute-start = (f32[40,128]{1,0:T(8,128)S(1)}, f32[40,128]{1,0:T(8,128)S(1)}, u32[]{:S(2)}, u32[]{:S(2)}) collective-permute-start(f32[40,128]{1,0:T(8,128)S(1)} %get-tuple-element.7.mine_ref), channel_id=1, source_target_pairs={{0,1},{1,0},{2,3},{3,2},{4,5},{5,4},{6,7},{7,6},{8,9},{9,8},{10,11... | collective-permute-start | bytes 61448 | tf_op jit(solution)/shard_map/ppermute | solution.py:267

commit v4 on v3

--- a/solution.py
+++ b/solution.py
@@ -10,25 +10,29 @@
 HALO = 8
 LANES = 128
 SHIFTS = 2 * HALO + 1
-OUTER, MIDDLE = 4, 2
-
-
-def exchange_order(count):
-    inner = count // (OUTER * MIDDLE)
+ALONG = (4, 2, 4, 2)
+
+
+def exchange_order():
+    ys, zs, xs, cores = ALONG
     return [
-        (outer * MIDDLE + middle) * inner + place
-        for outer in range(OUTER)
-        for place in range(inner)
-        for middle in range(MIDDLE)
+        ((y * zs + z) * xs + x) * cores + core
+        for core in range(cores)
+        for z in range(zs)
+        for y in range(ys)
+        for x in range(xs)
     ]
 
 
 def pack(coarse_ref, blocks_ref, sems):
-    local, outer, middle, inner = coarse_ref.shape[:4]
+    local, _, zs, _, cores = coarse_ref.shape[:5]
     copies = [
-        pltpu.make_async_copy(coarse_ref.at[s, :, m], blocks_ref.at[:, :, m, s], sems.at[s, m])
+        pltpu.make_async_copy(
+            coarse_ref.at[s, :, z, :, core], blocks_ref.at[core, z, :, :, s], sems.at[s, z, core]
+        )
         for s in range(local)
-        for m in range(middle)
+        for z in range(zs)
+        for core in range(cores)
     ]
     for copy in copies:
         copy.start()
@@ -38,12 +42,14 @@
 
 def write_taps(local, offsets_ref, taps_ref):
     spin_count, seg_count = offsets_ref.shape
-    middle, inner = MIDDLE, seg_count // local // (OUTER * MIDDLE)
+    ys, zs, xs, cores = ALONG
     source = lax.broadcasted_iota(jnp.int32, (seg_count, seg_count), 0)
     arrival = lax.broadcasted_iota(jnp.int32, (seg_count, seg_count), 1)
-    device, s = arrival // local, arrival % local
-    m, rest = device % middle, device // middle
-    natural = (((rest // inner) * middle + m) * inner + rest % inner) * local + s
+    s, device = arrival % local, arrival // local
+    x, device = device % xs, device // xs
+    y, device = device % ys, device // ys
+    z, core = device % zs, device // zs
+    natural = (((y * zs + z) * xs + x) * cores + core) * local + s
     move = jnp.where(source == natural, 1.0, 0.0).astype(jnp.bfloat16)
     arrived = jnp.dot(
         offsets_ref[...].astype(jnp.float32).astype(jnp.bfloat16), move, preferred_element_type=jnp.float32
@@ -53,7 +59,7 @@
         taps_ref[pl.ds(index * spin_count, spin_count), :] = jnp.where(hit, 1.0 / seg_count, 0.0).astype(jnp.bfloat16)
 
 
-def accumulate(local, offsets_ref, maps_ref, fine_ref, msg_ref, rest_ref, data, taps_ref, total, early, late, in_sems, out_sems):
+def accumulate(local, offsets_ref, maps_ref, fine_ref, msg_ref, rest_ref, data, taps_ref, total, early, late, in_sem, out_sems):
     spin_count, seg_count = offsets_ref.shape
     points = maps_ref.shape[0] // seg_count
     tiles = maps_ref.shape[1] // LANES
@@ -62,16 +68,20 @@
 
     def fetch(tile):
         return pltpu.make_async_copy(
-            maps_ref.at[:, pl.ds(tile * LANES, LANES)], data.at[tile], in_sems.at[tile]
-        )
+            maps_ref.at[:, pl.ds(tile * LANES, LANES)], data.at[tile], in_sem
+        )
+
+    def take(tile):
+        for row in range(0, seg_count * points, 8 * points):
+            data[tile, pl.ds(row, 8 * points), :] = maps_ref[pl.ds(row, 8 * points), tile * LANES : (tile + 1) * LANES]
 
     def emit(tile):
         return pltpu.make_async_copy(
             total.at[tile + 1], fine_ref.at[:, pl.ds(tile * LANES, LANES)], out_sems.at[tile]
         )
 
-    for tile in range(4):
-        fetch(tile).start()
+    take(0)
+    take(1)
     write_taps(local, offsets_ref, taps_ref)
     total[...] = jnp.zeros_like(total)
     lane = lax.broadcasted_iota(jnp.int32, (spin_count, LANES), 1)
@@ -116,20 +126,14 @@
                 where = pl.ds(group * 8 * points + point, 8, stride=points)
                 target[where, :] = target[where, :] + sums[place][group * 8 : group * 8 + 8]
 
-    def arrive(pair):
-        fetch(2 * pair).wait()
-        fetch(2 * pair + 1).wait()
-        if pair + 2 < pairs:
-            fetch(2 * pair + 4).start()
-            fetch(2 * pair + 5).start()
-
     half = points // 2
-    arrive(0)
     for point in range(half):
         multiply(0, point, early.at[point])
+    for tile in range(2, tiles - 1):
+        take(tile)
+    fetch(tiles - 1).start()
+    fetch(tiles - 1).wait()
     for pair in range(pairs):
-        if pair + 1 < pairs:
-            arrive(pair + 1)
         for point in range(half):
             multiply(pair, half + point, late.at[point])
             combine(pair, point, early.at[point])
@@ -222,26 +226,26 @@
     tiles = bins // LANES
     rows = spins * points
     groups = spins // 8
-    inner = nseg // (OUTER * MIDDLE)
+    ys, zs, xs, cores = ALONG
     vmem = pl.BlockSpec(memory_space=pltpu.VMEM)
     anywhere = pl.BlockSpec(memory_space=pl.ANY)
     mib = 1024 * 1024
     blocks = pl.pallas_call(
         pack,
-        out_shape=jax.ShapeDtypeStruct((OUTER, inner, MIDDLE, local_segs, points, bins), jnp.float32),
+        out_shape=jax.ShapeDtypeStruct((cores, zs, ys, xs, local_segs, points, bins), jnp.float32),
         in_specs=[anywhere],
         out_specs=vmem,
-        scratch_shapes=[pltpu.SemaphoreType.DMA((local_segs, MIDDLE))],
+        scratch_shapes=[pltpu.SemaphoreType.DMA((local_segs, zs, cores))],
         compiler_params=pltpu.CompilerParams(vmem_limit_bytes=44 * mib),
         name="pack",
-    )(coarse.reshape(local_segs, OUTER, MIDDLE, inner, points, bins))
+    )(coarse.reshape(local_segs, ys, zs, xs, cores, points, bins))
     maps = lax.all_to_all(
         blocks.reshape(nseg, local_segs, points, bins),
         "seg",
         split_axis=0,
         concat_axis=0,
         tiled=True,
-        axis_index_groups=[exchange_order(nseg)],
+        axis_index_groups=[exchange_order()],
     )
     fine, mine, rest = pl.pallas_call(
         functools.partial(accumulate, local_segs),
@@ -250,7 +254,7 @@
             jax.ShapeDtypeStruct(((groups + 1) * points, LANES), jnp.float32),
             jax.ShapeDtypeStruct((4, rows, LANES), jnp.float32),
         ),
-        in_specs=[vmem, anywhere],
+        in_specs=[vmem, vmem],
         out_specs=(anywhere, vmem, vmem),
         scratch_shapes=[
             pltpu.VMEM((tiles, segs * points, LANES), jnp.float32),
@@ -258,7 +262,7 @@
             pltpu.VMEM((tiles + 2, rows, LANES), jnp.float32),
             pltpu.VMEM((points // 2, SHIFTS * spins, 2 * LANES), jnp.float32),
             pltpu.VMEM((points // 2, SHIFTS * spins, 2 * LANES), jnp.float32),
-            pltpu.SemaphoreType.DMA((tiles,)),
+            pltpu.SemaphoreType.DMA,
             pltpu.SemaphoreType.DMA((tiles,)),
         ],
         compiler_params=pltpu.CompilerParams(vmem_limit_bytes=24 * mib),

time: 127 us -> 126 us (level)
  no operation moved by 1% of the time
where the time goes in v4:
time: 126 us
  blocking collectives  109 us (87%)
  Pallas kernels  12.3 us (10%)
  waiting for transfers between devices  2.78 us (2%)
    all_to_all x1, blocking collectives, on_device(): lax.all_to_all(blocks.reshape(nseg, local_segs, points, bins), 'seg', spl...  109 us
    pallas_call x1, Pallas kernels, on_device(): pl.pallas_call(functools.partial(accumulate, local_segs), out_shape=(jax....  7.41 us
    pallas_call x1, Pallas kernels, on_device(): pl.pallas_call(pack, out_shape=jax.ShapeDtypeStruct((cores, zs, ys, xs, l...  3.55 us
    ppermute x1, waiting for transfers between devices, on_device(): theirs = lax.ppermute(mine, 'freq', [(0, 1), (1, 0)])  2.78 us
  transfers between devices with their start and end apart: 1, of which 1 were waited for; matrix products, arithmetic and copies ran while one was open for 0% of the time, Pallas kernels for 0%

profile of v4, /device:TPU:0, one launch (start us, length us, event | category | flops | bytes accessed | tf_op | source)
XLA Modules:
  0.0 126.3 jit_solution(11579158567239608730)
XLA Ops:
  0.6 3.5 %pack.1 = f32[2,2,4,4,4,8,1024]{6,5,4,3,2,1,0:T(8,128)S(1)} custom-call(f32[4,4,2,4,2,8,1024]{6,5,4,3,2,1,0:T(8,128)} %bitcast.9), custom_call_target="tpu_custom_call" | custom-call | tf_op jit(solution)/shard_map/pack/pallas_call | solution.py:233
  4.2 0.0 copy-start
  4.2 109.4 %all_to_all.5 = f32[64,4,8,1024]{3,2,1,0:T(8,128)S(1)} all-to-all(f32[64,4,8,1024]{3,2,1,0:T(8,128)S(1)} %bitcast.7), channel_id=1, replica_groups={{0,4,8,12,32,36,40,44,64,68,72,76,96,100,104,108,16,20,24,28,48,52,56,6..., dimensions={0} | all-to-all | bytes 16777216 | tf_op jit(solution)/shard_map/all_to_all | solution.py:242
  113.6 0.0 copy-done
  113.6 7.4 %accumulate.1 = (f32[256,1024]{1,0:T(8,128)}, f32[40,128]{1,0:T(8,128)S(1)}, f32[4,256,128]{2,1,0:T(8,128)S(1)}) custom-call(s32[32,256]{1,0:T(8,128)S(1)} %bitcast.8, f32[2048,1024]{1,0:T(8,128)S(1)} %bitcast.6), custom_call_target="tpu_custom_call" | custom-call | tf_op jit(solution)/shard_map/accumulate/pallas_call | solution.py:250
  121.0 1.1 collective-permute-start
  122.1 2.8 %collective-permute-done.theirs_ref = f32[40,128]{1,0:T(8,128)S(1)} collective-permute-done((f32[40,128]{1,0:T(8,128)S(1)}, f32[40,128]{1,0:T(8,128)S(1)}, u32[]{:S(2)}, u32[]{:S(2)}) %collective-permute-start) | collective-permute-done | bytes 20512 | tf_op jit(solution)/shard_map/ppermute | solution.py:271
  124.9 1.4 %finish.1 = (f32[256,1024]{1,0:T(8,128)}, f32[1,8]{1,0:T(1,128)}) custom-call(f32[40,128]{1,0:T(8,128)S(1)} %get-tuple-element.7.mine_ref, f32[40,128]{1,0:T(8,128)S(1)} %collective-permute-done.theirs_ref, f32[4,256,128]{2,1,0:T(8,128)S(1)} %get-tuple-element.8.rest_ref, f32[256,1024]{1,0:T(8,128)} %get-tuple-element.9.fine_in), custom_call_target="tpu_custom_call", output_to_operand_aliasing={{0}: (3, {})} | custom-call | tf_op jit(solution)/shard_map/finish/pallas_call | solution.py:272
Async XLA Ops:
  4.2 109.4 %copy-start = (s32[256,32]{0,1:T(8,128)S(1)}, s32[256,32]{0,1:T(8,128)}, u32[]{:S(2)}) copy-start(s32[256,32]{0,1:T(8,128)} %param.3) | copy-start | bytes 98308
  121.0 3.9 %collective-permute-start = (f32[40,128]{1,0:T(8,128)S(1)}, f32[40,128]{1,0:T(8,128)S(1)}, u32[]{:S(2)}, u32[]{:S(2)}) collective-permute-start(f32[40,128]{1,0:T(8,128)S(1)} %get-tuple-element.7.mine_ref), channel_id=1, source_target_pairs={{0,1},{1,0},{2,3},{3,2},{4,5},{5,4},{6,7},{7,6},{8,9},{9,8},{10,11... | collective-permute-start | bytes 61448 | tf_op jit(solution)/shard_map/ppermute | solution.py:271

commit v5 on v4

--- a/solution.py
+++ b/solution.py
@@ -17,22 +17,19 @@
     ys, zs, xs, cores = ALONG
     return [
         ((y * zs + z) * xs + x) * cores + core
+        for y in range(ys)
+        for x in range(xs)
         for core in range(cores)
         for z in range(zs)
-        for y in range(ys)
-        for x in range(xs)
     ]
 
 
 def pack(coarse_ref, blocks_ref, sems):
-    local, _, zs, _, cores = coarse_ref.shape[:5]
+    local, _, zs = coarse_ref.shape[:3]
     copies = [
-        pltpu.make_async_copy(
-            coarse_ref.at[s, :, z, :, core], blocks_ref.at[core, z, :, :, s], sems.at[s, z, core]
-        )
+        pltpu.make_async_copy(coarse_ref.at[s, :, z], blocks_ref.at[:, :, z, s], sems.at[s, z])
         for s in range(local)
         for z in range(zs)
-        for core in range(cores)
     ]
     for copy in copies:
         copy.start()
@@ -46,9 +43,9 @@
     source = lax.broadcasted_iota(jnp.int32, (seg_count, seg_count), 0)
     arrival = lax.broadcasted_iota(jnp.int32, (seg_count, seg_count), 1)
     s, device = arrival % local, arrival // local
-    x, device = device % xs, device // xs
-    y, device = device % ys, device // ys
-    z, core = device % zs, device // zs
+    z, device = device % zs, device // zs
+    core, device = device % cores, device // cores
+    x, y = device % xs, device // xs
     natural = (((y * zs + z) * xs + x) * cores + core) * local + s
     move = jnp.where(source == natural, 1.0, 0.0).astype(jnp.bfloat16)
     arrived = jnp.dot(
@@ -232,13 +229,13 @@
     mib = 1024 * 1024
     blocks = pl.pallas_call(
         pack,
-        out_shape=jax.ShapeDtypeStruct((cores, zs, ys, xs, local_segs, points, bins), jnp.float32),
+        out_shape=jax.ShapeDtypeStruct((ys, xs * cores, zs, local_segs, points, bins), jnp.float32),
         in_specs=[anywhere],
         out_specs=vmem,
-        scratch_shapes=[pltpu.SemaphoreType.DMA((local_segs, zs, cores))],
+        scratch_shapes=[pltpu.SemaphoreType.DMA((local_segs, zs))],
         compiler_params=pltpu.CompilerParams(vmem_limit_bytes=44 * mib),
         name="pack",
-    )(coarse.reshape(local_segs, ys, zs, xs, cores, points, bins))
+    )(coarse.reshape(local_segs, ys, zs, xs * cores, points, bins))
     maps = lax.all_to_all(
         blocks.reshape(nseg, local_segs, points, bins),
         "seg",

time: 126 us -> 126 us (level)
  no operation moved by 1% of the time
where the time goes in v5:
time: 126 us
  blocking collectives  109 us (87%)
  Pallas kernels  12.2 us (10%)
  waiting for transfers between devices  2.75 us (2%)
    all_to_all x1, blocking collectives, on_device(): lax.all_to_all(blocks.reshape(nseg, local_segs, points, bins), 'seg', spl...  109 us
    pallas_call x1, Pallas kernels, on_device(): pl.pallas_call(functools.partial(accumulate, local_segs), out_shape=(jax....  7.4 us
    pallas_call x1, Pallas kernels, on_device(): pl.pallas_call(pack, out_shape=jax.ShapeDtypeStruct((ys, xs * cores, zs,...  3.49 us
    ppermute x1, waiting for transfers between devices, on_device(): theirs = lax.ppermute(mine, 'freq', [(0, 1), (1, 0)])  2.75 us
  transfers between devices with their start and end apart: 1, of which 1 were waited for; matrix products, arithmetic and copies ran while one was open for 0% of the time, Pallas kernels for 0%

profile of v5, /device:TPU:0, one launch (start us, length us, event | category | flops | bytes accessed | tf_op | source)
XLA Modules:
  0.0 126.1 jit_solution(13187590504111954050)
XLA Ops:
  0.6 3.5 %pack.1 = f32[4,8,2,4,8,1024]{5,4,3,2,1,0:T(8,128)S(1)} custom-call(f32[4,4,2,8,8,1024]{5,4,3,2,1,0:T(8,128)} %bitcast.9), custom_call_target="tpu_custom_call" | custom-call | tf_op jit(solution)/shard_map/pack/pallas_call | solution.py:230
  4.1 0.0 copy-start
  4.1 109.3 %all_to_all.5 = f32[64,4,8,1024]{3,2,1,0:T(8,128)S(1)} all-to-all(f32[64,4,8,1024]{3,2,1,0:T(8,128)S(1)} %bitcast.7), channel_id=1, replica_groups={{0,16,2,18,4,20,6,22,8,24,10,26,12,28,14,30,32,48,34,50,36,52,38,54,40,..., dimensions={0} | all-to-all | bytes 16777216 | tf_op jit(solution)/shard_map/all_to_all | solution.py:239
  113.4 0.0 copy-done
  113.4 7.4 %accumulate.1 = (f32[256,1024]{1,0:T(8,128)}, f32[40,128]{1,0:T(8,128)S(1)}, f32[4,256,128]{2,1,0:T(8,128)S(1)}) custom-call(s32[32,256]{1,0:T(8,128)S(1)} %bitcast.8, f32[2048,1024]{1,0:T(8,128)S(1)} %bitcast.6), custom_call_target="tpu_custom_call" | custom-call | tf_op jit(solution)/shard_map/accumulate/pallas_call | solution.py:247
  120.8 1.1 collective-permute-start
  122.0 2.8 %collective-permute-done.theirs_ref = f32[40,128]{1,0:T(8,128)S(1)} collective-permute-done((f32[40,128]{1,0:T(8,128)S(1)}, f32[40,128]{1,0:T(8,128)S(1)}, u32[]{:S(2)}, u32[]{:S(2)}) %collective-permute-start) | collective-permute-done | bytes 20512 | tf_op jit(solution)/shard_map/ppermute | solution.py:268
  124.7 1.4 %finish.1 = (f32[256,1024]{1,0:T(8,128)}, f32[1,8]{1,0:T(1,128)}) custom-call(f32[40,128]{1,0:T(8,128)S(1)} %get-tuple-element.7.mine_ref, f32[40,128]{1,0:T(8,128)S(1)} %collective-permute-done.theirs_ref, f32[4,256,128]{2,1,0:T(8,128)S(1)} %get-tuple-element.8.rest_ref, f32[256,1024]{1,0:T(8,128)} %get-tuple-element.9.fine_in), custom_call_target="tpu_custom_call", output_to_operand_aliasing={{0}: (3, {})} | custom-call | tf_op jit(solution)/shard_map/finish/pallas_call | solution.py:269
Async XLA Ops:
  4.1 109.3 %copy-start = (s32[256,32]{0,1:T(8,128)S(1)}, s32[256,32]{0,1:T(8,128)}, u32[]{:S(2)}) copy-start(s32[256,32]{0,1:T(8,128)} %param.3) | copy-start | bytes 98308
  120.8 3.9 %collective-permute-start = (f32[40,128]{1,0:T(8,128)S(1)}, f32[40,128]{1,0:T(8,128)S(1)}, u32[]{:S(2)}, u32[]{:S(2)}) collective-permute-start(f32[40,128]{1,0:T(8,128)S(1)} %get-tuple-element.7.mine_ref), channel_id=1, source_target_pairs={{0,1},{1,0},{2,3},{3,2},{4,5},{5,4},{6,7},{7,6},{8,9},{9,8},{10,11... | collective-permute-start | bytes 61448 | tf_op jit(solution)/shard_map/ppermute | solution.py:268

commit v6 on v5

--- a/solution.py
+++ b/solution.py
@@ -81,7 +81,7 @@
     take(1)
     write_taps(local, offsets_ref, taps_ref)
     total[...] = jnp.zeros_like(total)
-    lane = lax.broadcasted_iota(jnp.int32, (spin_count, LANES), 1)
+    lane = lax.broadcasted_iota(jnp.int32, (8, LANES), 1)
 
     def multiply(pair, point, product):
         block = jnp.concatenate(
@@ -96,41 +96,41 @@
         )
 
     def combine(pair, point, product):
-        sums = [jnp.zeros((spin_count, LANES), jnp.float32) for _ in range(4)]
-        for index in range(SHIFTS):
-            shift = index - HALO
-            where = pl.ds(index * spin_count, spin_count)
-            left, right = product[where, :LANES], product[where, LANES:]
-            if shift == 0:
-                sums[1] = sums[1] + left
-                sums[2] = sums[2] + right
-                continue
-            left = pltpu.roll(left, (-shift) % LANES, 1)
-            right = pltpu.roll(right, (-shift) % LANES, 1)
-            if shift > 0:
-                same = lane < LANES - shift
-                sums[0] = sums[0] + jnp.where(same, 0.0, left)
-                sums[1] = sums[1] + jnp.where(same, left, right)
-                sums[2] = sums[2] + jnp.where(same, right, 0.0)
-            else:
-                same = lane >= -shift
-                sums[1] = sums[1] + jnp.where(same, left, 0.0)
-                sums[2] = sums[2] + jnp.where(same, right, left)
-                sums[3] = sums[3] + jnp.where(same, 0.0, right)
-        for place in range(4):
-            target = total.at[2 * pair + place]
-            for group in range(groups):
-                where = pl.ds(group * 8 * points + point, 8, stride=points)
-                target[where, :] = target[where, :] + sums[place][group * 8 : group * 8 + 8]
+        for group in range(groups):
+            sums = [jnp.zeros((8, LANES), jnp.float32) for _ in range(4)]
+            for index in range(SHIFTS):
+                shift = index - HALO
+                where = pl.ds(index * spin_count + 8 * group, 8)
+                left, right = product[where, :LANES], product[where, LANES:]
+                if shift == 0:
+                    sums[1] = sums[1] + left
+                    sums[2] = sums[2] + right
+                    continue
+                left = pltpu.roll(left, (-shift) % LANES, 1)
+                right = pltpu.roll(right, (-shift) % LANES, 1)
+                if shift > 0:
+                    same = lane < LANES - shift
+                    sums[0] = sums[0] + jnp.where(same, 0.0, left)
+                    sums[1] = sums[1] + jnp.where(same, left, right)
+                    sums[2] = sums[2] + jnp.where(same, right, 0.0)
+                else:
+                    same = lane >= -shift
+                    sums[1] = sums[1] + jnp.where(same, left, 0.0)
+                    sums[2] = sums[2] + jnp.where(same, right, left)
+                    sums[3] = sums[3] + jnp.where(same, 0.0, right)
+            where = pl.ds(group * 8 * points + point, 8, stride=points)
+            for place in range(4):
+                target = total.at[2 * pair + place]
+                target[where, :] = target[where, :] + sums[place]
 
     half = points // 2
     for point in range(half):
         multiply(0, point, early.at[point])
-    for tile in range(2, tiles - 1):
-        take(tile)
     fetch(tiles - 1).start()
     fetch(tiles - 1).wait()
     for pair in range(pairs):
+        for tile in range(2 * pair + 2, min(2 * pair + 4, tiles - 1)):
+            take(tile)
         for point in range(half):
             multiply(pair, half + point, late.at[point])
             combine(pair, point, early.at[point])

time: 126 us -> 126 us (level)
  no operation moved by 1% of the time
where the time goes in v6:
time: 126 us; the launch traced here: 125 us
  blocking collectives  109 us (87%)
  Pallas kernels  11.6 us (9%)
  waiting for transfers between devices  2.77 us (2%)
    all_to_all x1, blocking collectives, on_device(): lax.all_to_all(blocks.reshape(nseg, local_segs, points, bins), 'seg', spl...  109 us
    pallas_call x1, Pallas kernels, on_device(): pl.pallas_call(functools.partial(accumulate, local_segs), out_shape=(jax....  6.76 us
    pallas_call x1, Pallas kernels, on_device(): pl.pallas_call(pack, out_shape=jax.ShapeDtypeStruct((ys, xs * cores, zs,...  3.49 us
    ppermute x1, waiting for transfers between devices, on_device(): theirs = lax.ppermute(mine, 'freq', [(0, 1), (1, 0)])  2.77 us
  transfers between devices with their start and end apart: 1, of which 1 were waited for; matrix products, arithmetic and copies ran while one was open for 0% of the time, Pallas kernels for 0%

profile of v6, /device:TPU:0, one launch (start us, length us, event | category | flops | bytes accessed | tf_op | source)
XLA Modules:
  0.0 125.4 jit_solution(7751791204860159374)
XLA Ops:
  0.6 3.5 %pack.1 = f32[4,8,2,4,8,1024]{5,4,3,2,1,0:T(8,128)S(1)} custom-call(f32[4,4,2,8,8,1024]{5,4,3,2,1,0:T(8,128)} %bitcast.9), custom_call_target="tpu_custom_call" | custom-call | tf_op jit(solution)/shard_map/pack/pallas_call | solution.py:230
  4.1 0.0 copy-start
  4.1 109.3 %all_to_all.5 = f32[64,4,8,1024]{3,2,1,0:T(8,128)S(1)} all-to-all(f32[64,4,8,1024]{3,2,1,0:T(8,128)S(1)} %bitcast.7), channel_id=1, replica_groups={{0,16,2,18,4,20,6,22,8,24,10,26,12,28,14,30,32,48,34,50,36,52,38,54,40,..., dimensions={0} | all-to-all | bytes 16777216 | tf_op jit(solution)/shard_map/all_to_all | solution.py:239
  113.4 0.0 copy-done
  113.4 6.8 %accumulate.1 = (f32[256,1024]{1,0:T(8,128)}, f32[40,128]{1,0:T(8,128)S(1)}, f32[4,256,128]{2,1,0:T(8,128)S(1)}) custom-call(s32[32,256]{1,0:T(8,128)S(1)} %bitcast.8, f32[2048,1024]{1,0:T(8,128)S(1)} %bitcast.6), custom_call_target="tpu_custom_call" | custom-call | tf_op jit(solution)/shard_map/accumulate/pallas_call | solution.py:247
  120.2 1.1 collective-permute-start
  121.3 2.8 %collective-permute-done.theirs_ref = f32[40,128]{1,0:T(8,128)S(1)} collective-permute-done((f32[40,128]{1,0:T(8,128)S(1)}, f32[40,128]{1,0:T(8,128)S(1)}, u32[]{:S(2)}, u32[]{:S(2)}) %collective-permute-start) | collective-permute-done | bytes 20512 | tf_op jit(solution)/shard_map/ppermute | solution.py:268
  124.1 1.4 %finish.1 = (f32[256,1024]{1,0:T(8,128)}, f32[1,8]{1,0:T(1,128)}) custom-call(f32[40,128]{1,0:T(8,128)S(1)} %get-tuple-element.7.mine_ref, f32[40,128]{1,0:T(8,128)S(1)} %collective-permute-done.theirs_ref, f32[4,256,128]{2,1,0:T(8,128)S(1)} %get-tuple-element.8.rest_ref, f32[256,1024]{1,0:T(8,128)} %get-tuple-element.9.fine_in), custom_call_target="tpu_custom_call", output_to_operand_aliasing={{0}: (3, {})} | custom-call | tf_op jit(solution)/shard_map/finish/pallas_call | solution.py:269
Async XLA Ops:
  4.1 109.3 %copy-start = (s32[256,32]{0,1:T(8,128)S(1)}, s32[256,32]{0,1:T(8,128)}, u32[]{:S(2)}) copy-start(s32[256,32]{0,1:T(8,128)} %param.3) | copy-start | bytes 98308
  120.2 3.9 %collective-permute-start = (f32[40,128]{1,0:T(8,128)S(1)}, f32[40,128]{1,0:T(8,128)S(1)}, u32[]{:S(2)}, u32[]{:S(2)}) collective-permute-start(f32[40,128]{1,0:T(8,128)S(1)} %get-tuple-element.7.mine_ref), channel_id=1, source_target_pairs={{0,1},{1,0},{2,3},{3,2},{4,5},{5,4},{6,7},{7,6},{8,9},{9,8},{10,11... | collective-permute-start | bytes 61448 | tf_op jit(solution)/shard_map/ppermute | solution.py:268

commit v7 on v6

--- a/solution.py
+++ b/solution.py
@@ -19,15 +19,15 @@
         ((y * zs + z) * xs + x) * cores + core
         for y in range(ys)
         for x in range(xs)
+        for z in range(zs)
         for core in range(cores)
-        for z in range(zs)
     ]
 
 
 def pack(coarse_ref, blocks_ref, sems):
     local, _, zs = coarse_ref.shape[:3]
     copies = [
-        pltpu.make_async_copy(coarse_ref.at[s, :, z], blocks_ref.at[:, :, z, s], sems.at[s, z])
+        pltpu.make_async_copy(coarse_ref.at[s, :, z], blocks_ref.at[:, :, z, :, s], sems.at[s, z])
         for s in range(local)
         for z in range(zs)
     ]
@@ -43,8 +43,8 @@
     source = lax.broadcasted_iota(jnp.int32, (seg_count, seg_count), 0)
     arrival = lax.broadcasted_iota(jnp.int32, (seg_count, seg_count), 1)
     s, device = arrival % local, arrival // local
+    core, device = device % cores, device // cores
     z, device = device % zs, device // zs
-    core, device = device % cores, device // cores
     x, y = device % xs, device // xs
     natural = (((y * zs + z) * xs + x) * cores + core) * local + s
     move = jnp.where(source == natural, 1.0, 0.0).astype(jnp.bfloat16)
@@ -229,13 +229,13 @@
     mib = 1024 * 1024
     blocks = pl.pallas_call(
         pack,
-        out_shape=jax.ShapeDtypeStruct((ys, xs * cores, zs, local_segs, points, bins), jnp.float32),
+        out_shape=jax.ShapeDtypeStruct((ys, xs, zs, cores, local_segs, points, bins), jnp.float32),
         in_specs=[anywhere],
         out_specs=vmem,
         scratch_shapes=[pltpu.SemaphoreType.DMA((local_segs, zs))],
         compiler_params=pltpu.CompilerParams(vmem_limit_bytes=44 * mib),
         name="pack",
-    )(coarse.reshape(local_segs, ys, zs, xs * cores, points, bins))
+    )(coarse.reshape(local_segs, ys, zs, xs, cores, points, bins))
     maps = lax.all_to_all(
         blocks.reshape(nseg, local_segs, points, bins),
         "seg",

time: 126 us -> 125 us (level)
  no operation moved by 1% of the time
where the time goes in v7:
time: 125 us
  blocking collectives  109 us (87%)
  Pallas kernels  11.6 us (9%)
  waiting for transfers between devices  2.76 us (2%)
    all_to_all x1, blocking collectives, on_device(): lax.all_to_all(blocks.reshape(nseg, local_segs, points, bins), 'seg', spl...  109 us
    pallas_call x1, Pallas kernels, on_device(): pl.pallas_call(functools.partial(accumulate, local_segs), out_shape=(jax....  6.76 us
    pallas_call x1, Pallas kernels, on_device(): pl.pallas_call(pack, out_shape=jax.ShapeDtypeStruct((ys, xs, zs, cores, l...  3.49 us
    ppermute x1, waiting for transfers between devices, on_device(): theirs = lax.ppermute(mine, 'freq', [(0, 1), (1, 0)])  2.76 us
  transfers between devices with their start and end apart: 1, of which 1 were waited for; matrix products, arithmetic and copies ran while one was open for 0% of the time, Pallas kernels for 0%

profile of v7, /device:TPU:0, one launch (start us, length us, event | category | flops | bytes accessed | tf_op | source)
XLA Modules:
  0.0 125.0 jit_solution(16083547649116308851)
XLA Ops:
  0.6 3.5 %pack.1 = f32[4,4,2,2,4,8,1024]{6,5,4,3,2,1,0:T(8,128)S(1)} custom-call(f32[4,4,2,4,2,8,1024]{6,5,4,3,2,1,0:T(8,128)} %bitcast.9), custom_call_target="tpu_custom_call" | custom-call | tf_op jit(solution)/shard_map/pack/pallas_call | solution.py:230
  4.1 0.0 copy-start
  4.1 108.9 %all_to_all.5 = f32[64,4,8,1024]{3,2,1,0:T(8,128)S(1)} all-to-all(f32[64,4,8,1024]{3,2,1,0:T(8,128)S(1)} %bitcast.7), channel_id=1, replica_groups={{0,2,16,18,4,6,20,22,8,10,24,26,12,14,28,30,32,34,48,50,36,38,52,54,40,..., dimensions={0} | all-to-all | bytes 16777216 | tf_op jit(solution)/shard_map/all_to_all | solution.py:239
  113.0 0.0 copy-done
  113.0 6.8 %accumulate.1 = (f32[256,1024]{1,0:T(8,128)}, f32[40,128]{1,0:T(8,128)S(1)}, f32[4,256,128]{2,1,0:T(8,128)S(1)}) custom-call(s32[32,256]{1,0:T(8,128)S(1)} %bitcast.8, f32[2048,1024]{1,0:T(8,128)S(1)} %bitcast.6), custom_call_target="tpu_custom_call" | custom-call | tf_op jit(solution)/shard_map/accumulate/pallas_call | solution.py:247
  119.8 1.1 collective-permute-start
  120.9 2.8 %collective-permute-done.theirs_ref = f32[40,128]{1,0:T(8,128)S(1)} collective-permute-done((f32[40,128]{1,0:T(8,128)S(1)}, f32[40,128]{1,0:T(8,128)S(1)}, u32[]{:S(2)}, u32[]{:S(2)}) %collective-permute-start) | collective-permute-done | bytes 20512 | tf_op jit(solution)/shard_map/ppermute | solution.py:268
  123.7 1.4 %finish.1 = (f32[256,1024]{1,0:T(8,128)}, f32[1,8]{1,0:T(1,128)}) custom-call(f32[40,128]{1,0:T(8,128)S(1)} %get-tuple-element.7.mine_ref, f32[40,128]{1,0:T(8,128)S(1)} %collective-permute-done.theirs_ref, f32[4,256,128]{2,1,0:T(8,128)S(1)} %get-tuple-element.8.rest_ref, f32[256,1024]{1,0:T(8,128)} %get-tuple-element.9.fine_in), custom_call_target="tpu_custom_call", output_to_operand_aliasing={{0}: (3, {})} | custom-call | tf_op jit(solution)/shard_map/finish/pallas_call | solution.py:269
Async XLA Ops:
  4.1 108.9 %copy-start = (s32[256,32]{0,1:T(8,128)S(1)}, s32[256,32]{0,1:T(8,128)}, u32[]{:S(2)}) copy-start(s32[256,32]{0,1:T(8,128)} %param.3) | copy-start | bytes 98308
  119.8 3.9 %collective-permute-start = (f32[40,128]{1,0:T(8,128)S(1)}, f32[40,128]{1,0:T(8,128)S(1)}, u32[]{:S(2)}, u32[]{:S(2)}) collective-permute-start(f32[40,128]{1,0:T(8,128)S(1)} %get-tuple-element.7.mine_ref), channel_id=1, source_target_pairs={{0,1},{1,0},{2,3},{3,2},{4,5},{5,4},{6,7},{7,6},{8,9},{9,8},{10,11... | collective-permute-start | bytes 61448 | tf_op jit(solution)/shard_map/ppermute | solution.py:268

commit v8 on v7

--- a/solution.py
+++ b/solution.py
@@ -18,18 +18,21 @@
     return [
         ((y * zs + z) * xs + x) * cores + core
         for y in range(ys)
+        for core in range(cores)
         for x in range(xs)
         for z in range(zs)
-        for core in range(cores)
     ]
 
 
 def pack(coarse_ref, blocks_ref, sems):
-    local, _, zs = coarse_ref.shape[:3]
+    local, _, zs, _, cores = coarse_ref.shape[:5]
     copies = [
-        pltpu.make_async_copy(coarse_ref.at[s, :, z], blocks_ref.at[:, :, z, :, s], sems.at[s, z])
+        pltpu.make_async_copy(
+            coarse_ref.at[s, :, z, :, core], blocks_ref.at[:, core, :, z, s], sems.at[s, z, core]
+        )
         for s in range(local)
         for z in range(zs)
+        for core in range(cores)
     ]
     for copy in copies:
         copy.start()
@@ -43,9 +46,9 @@
     source = lax.broadcasted_iota(jnp.int32, (seg_count, seg_count), 0)
     arrival = lax.broadcasted_iota(jnp.int32, (seg_count, seg_count), 1)
     s, device = arrival % local, arrival // local
-    core, device = device % cores, device // cores
     z, device = device % zs, device // zs
-    x, y = device % xs, device // xs
+    x, device = device % xs, device // xs
+    core, y = device % cores, device // cores
     natural = (((y * zs + z) * xs + x) * cores + core) * local + s
     move = jnp.where(source == natural, 1.0, 0.0).astype(jnp.bfloat16)
     arrived = jnp.dot(
@@ -229,10 +232,10 @@
     mib = 1024 * 1024
     blocks = pl.pallas_call(
         pack,
-        out_shape=jax.ShapeDtypeStruct((ys, xs, zs, cores, local_segs, points, bins), jnp.float32),
+        out_shape=jax.ShapeDtypeStruct((ys, cores, xs, zs, local_segs, points, bins), jnp.float32),
         in_specs=[anywhere],
         out_specs=vmem,
-        scratch_shapes=[pltpu.SemaphoreType.DMA((local_segs, zs))],
+        scratch_shapes=[pltpu.SemaphoreType.DMA((local_segs, zs, cores))],
         compiler_params=pltpu.CompilerParams(vmem_limit_bytes=44 * mib),
         name="pack",
     )(coarse.reshape(local_segs, ys, zs, xs, cores, points, bins))

time: 125 us -> 126 us (level)
  no operation moved by 1% of the time
where the time goes in v8:
time: 126 us
  blocking collectives  109 us (87%)
  Pallas kernels  11.7 us (9%)
  waiting for transfers between devices  2.76 us (2%)
    all_to_all x1, blocking collectives, on_device(): lax.all_to_all(blocks.reshape(nseg, local_segs, points, bins), 'seg', spl...  109 us
    pallas_call x1, Pallas kernels, on_device(): pl.pallas_call(functools.partial(accumulate, local_segs), out_shape=(jax....  6.75 us
    pallas_call x1, Pallas kernels, on_device(): pl.pallas_call(pack, out_shape=jax.ShapeDtypeStruct((ys, cores, xs, zs, l...  3.55 us
    ppermute x1, waiting for transfers between devices, on_device(): theirs = lax.ppermute(mine, 'freq', [(0, 1), (1, 0)])  2.76 us
  transfers between devices with their start and end apart: 1, of which 1 were waited for; matrix products, arithmetic and copies ran while one was open for 0% of the time, Pallas kernels for 0%

profile of v8, /device:TPU:0, one launch (start us, length us, event | category | flops | bytes accessed | tf_op | source)
XLA Modules:
  0.0 125.6 jit_solution(16671310155141875780)
XLA Ops:
  0.6 3.5 %pack.1 = f32[4,2,4,2,4,8,1024]{6,5,4,3,2,1,0:T(8,128)S(1)} custom-call(f32[4,4,2,4,2,8,1024]{6,5,4,3,2,1,0:T(8,128)} %bitcast.9), custom_call_target="tpu_custom_call" | custom-call | tf_op jit(solution)/shard_map/pack/pallas_call | solution.py:233
  4.2 0.0 copy-start
  4.2 109.4 %all_to_all.5 = f32[64,4,8,1024]{3,2,1,0:T(8,128)S(1)} all-to-all(f32[64,4,8,1024]{3,2,1,0:T(8,128)S(1)} %bitcast.7), channel_id=1, replica_groups={{0,16,4,20,8,24,12,28,2,18,6,22,10,26,14,30,32,48,36,52,40,56,44,60,34,..., dimensions={0} | all-to-all | bytes 16777216 | tf_op jit(solution)/shard_map/all_to_all | solution.py:242
  113.6 0.0 copy-done
  113.6 6.8 %accumulate.1 = (f32[256,1024]{1,0:T(8,128)}, f32[40,128]{1,0:T(8,128)S(1)}, f32[4,256,128]{2,1,0:T(8,128)S(1)}) custom-call(s32[32,256]{1,0:T(8,128)S(1)} %bitcast.8, f32[2048,1024]{1,0:T(8,128)S(1)} %bitcast.6), custom_call_target="tpu_custom_call" | custom-call | tf_op jit(solution)/shard_map/accumulate/pallas_call | solution.py:250
  120.4 1.1 collective-permute-start
  121.5 2.8 %collective-permute-done.theirs_ref = f32[40,128]{1,0:T(8,128)S(1)} collective-permute-done((f32[40,128]{1,0:T(8,128)S(1)}, f32[40,128]{1,0:T(8,128)S(1)}, u32[]{:S(2)}, u32[]{:S(2)}) %collective-permute-start) | collective-permute-done | bytes 20512 | tf_op jit(solution)/shard_map/ppermute | solution.py:271
  124.2 1.4 %finish.1 = (f32[256,1024]{1,0:T(8,128)}, f32[1,8]{1,0:T(1,128)}) custom-call(f32[40,128]{1,0:T(8,128)S(1)} %get-tuple-element.7.mine_ref, f32[40,128]{1,0:T(8,128)S(1)} %collective-permute-done.theirs_ref, f32[4,256,128]{2,1,0:T(8,128)S(1)} %get-tuple-element.8.rest_ref, f32[256,1024]{1,0:T(8,128)} %get-tuple-element.9.fine_in), custom_call_target="tpu_custom_call", output_to_operand_aliasing={{0}: (3, {})} | custom-call | tf_op jit(solution)/shard_map/finish/pallas_call | solution.py:272
Async XLA Ops:
  4.2 109.4 %copy-start = (s32[256,32]{0,1:T(8,128)S(1)}, s32[256,32]{0,1:T(8,128)}, u32[]{:S(2)}) copy-start(s32[256,32]{0,1:T(8,128)} %param.3) | copy-start | bytes 98308
  120.4 3.9 %collective-permute-start = (f32[40,128]{1,0:T(8,128)S(1)}, f32[40,128]{1,0:T(8,128)S(1)}, u32[]{:S(2)}, u32[]{:S(2)}) collective-permute-start(f32[40,128]{1,0:T(8,128)S(1)} %get-tuple-element.7.mine_ref), channel_id=1, source_target_pairs={{0,1},{1,0},{2,3},{3,2},{4,5},{5,4},{6,7},{7,6},{8,9},{9,8},{10,11... | collective-permute-start | bytes 61448 | tf_op jit(solution)/shard_map/ppermute | solution.py:271
